TPU v7x, 512 devices: a whole 4x8x8 slice. The times are simulated.
512 devices in a mesh: grp: 8 (over z), dev: 64 (over x, y, core).
Axes of the slice: x: 4, y: 8, z: 8, core: 2. Of those that a mesh axis runs over, the one named last changes fastest.
Arguments:
- points: float32 [524288, 768], P(('grp', 'dev')), may hold values from -12 to 12
- assignment: int32 [524288], P(('grp', 'dev')), may hold values from 0 to 16383, as said below
Outputs:
- centroids: float32 [16384, 768], P('dev')
- spread: float32 [16384], P('dev')
Inputs may be any that keep to these rules, and one draw needn't show every extreme that they name: `assignment`: the owner of cluster c is c // 256. Among the 1024 points of one device (aligned blocks of 1024), at most 32 belong to clusters of one owner; some owner receives exactly 32 from every device's block.
All inputs are finite; a program needn't handle non-finite values.
Results may differ from a plain program's by a relative error of at most 0.000071.
Values sent between devices are 32-bit elements; how exact they have to be, the bound alone decides.
No kernel may reach another device: no remote copies, remote signals or barrier semaphores. Data moves between devices by JAX's collectives and lax.ppermute only.
A program may use at most 64 MiB of HBM per device.

v0:
```python
import math

import jax
import jax.numpy as jnp
from jax import lax
from jax.sharding import PartitionSpec as P

CL_OWN = 256


def cut_along(value, dim, peers):
    before, after = (value.shape[:dim], value.shape[dim + 1 :])
    return jnp.moveaxis(value.reshape(*before, peers, -1, *after), dim, 0)


def sum_at_owner(value, axis, dim):
    parts = cut_along(value, dim, lax.axis_size(axis))
    arrived = lax.all_to_all(parts, axis, split_axis=0, concat_axis=0, tiled=True)
    return arrived.sum(axis=0)


def sent_together(arrays, axis, dim, along):
    widths = [math.prod(a.shape[along:]) for a in arrays]
    both = jnp.concatenate(
        [a.reshape(*a.shape[:along], w) for a, w in zip(arrays, widths)], axis=along
    )
    out = sum_at_owner(both, axis, dim)
    parts = jnp.split(out, [sum(widths[:k]) for k in range(1, len(widths))], axis=along)
    return tuple((b.reshape(*out.shape[:along], *a.shape[along:]) for a, b in zip(arrays, parts)))


def in_one_piece(arrays, axis, dim, along):
    columns = [a.reshape(*a.shape[:along], -1) for a in arrays]
    both = jnp.concatenate(columns, axis=along)
    out, at, done = (lax.all_gather(both, axis, axis=dim, tiled=True), 0, [])
    for a, column in zip(arrays, columns):
        piece = out[..., at : at + column.shape[along]]
        done.append(piece.reshape(*piece.shape[:along], *a.shape[along:]))
        at += column.shape[along]
    return tuple(done)


def finish(sums, counts, squares):
    denom = jnp.maximum(counts, 1.0)
    centre = sums / denom[:, None]
    spread = (squares - jnp.sum(sums * sums, axis=1) / denom) / (denom * sums.shape[1])
    return (centre, spread)


def body(points, assignment):
    owners = lax.axis_size("dev")
    rows, width = points.shape
    capacity = 2 * rows // owners
    owner = assignment // CL_OWN
    local_label = assignment % CL_OWN
    matches = (owner[:, None] == jnp.arange(owners, dtype=jnp.int32)[None, :]).astype(jnp.float32)
    earlier = (jnp.arange(rows)[:, None] > jnp.arange(rows)[None, :]).astype(jnp.float32)
    before = jnp.dot(earlier, matches, preferred_element_type=jnp.float32)
    position = jnp.sum(before * matches, axis=1).astype(jnp.int32)
    target = owner * capacity + position
    outgoing = jnp.zeros((owners * capacity, width), jnp.float32).at[target].set(points)
    labels = jnp.full((owners * capacity,), -1, jnp.int32).at[target].set(local_label)
    arrived, tags = (
        lax.all_to_all(
            outgoing.reshape(owners, capacity, width),
            "dev",
            split_axis=0,
            concat_axis=0,
            tiled=True,
        ),
        lax.all_to_all(
            labels.reshape(owners, capacity), "dev", split_axis=0, concat_axis=0, tiled=True
        ),
    )
    arrived = arrived.reshape(owners * capacity, width)
    tags = tags.reshape(owners * capacity)
    onehot = (jnp.arange(CL_OWN, dtype=jnp.int32)[:, None] == tags[None, :]).astype(jnp.float32)
    sums = jnp.dot(
        onehot, arrived, precision=lax.Precision.HIGHEST, preferred_element_type=jnp.float32
    )
    counts = jnp.sum(onehot, axis=1)
    squares = jnp.dot(
        onehot,
        jnp.sum(arrived * arrived, axis=1),
        precision=lax.Precision.HIGHEST,
        preferred_element_type=jnp.float32,
    )
    sums, counts, squares = sent_together((sums, counts, squares), "grp", 0, 1)
    centre, spread = finish(sums, counts, squares)
    centre, spread = in_one_piece((centre, spread), "grp", 0, 1)
    return (centre, spread)


def solution(mesh):
    return jax.shard_map(
        body,
        mesh=mesh,
        in_specs=(P(("grp", "dev"), None), P(("grp", "dev"))),
        out_specs=(P("dev", None), P("dev")),
        check_vma=False,
    )
```

profile of v0, /device:TPU:2, one launch (start us, length us, event | category | flops | bytes accessed | tf_op | source)
XLA Modules:
  0.0 253.8 jit_solution(6939519142803837594)
XLA Ops:
  0.6 0.7 add_select_fusion.1
  1.3 0.6 fusion.8
  1.9 0.7 add_select_fusion
  2.6 4.3 %scatter_custom_fusion = s32[2048]{0:T(1024)S(1)} fusion(s32[1024]{0:T(1024)S(1)} %get-tuple-element.9, s32[1024]{0:T(1024)S(1)} %get-tuple-element.8, s32[]{:T(128)} %constant.34.clone.1), kind=kCustom, calls=%fused_computation.38 | custom fusion | bytes 8196 | tf_op jit(solution)/shard_map/scatter | solution.py:62
  7.0 0.7 all_to_all.12
  7.6 10.7 %all-to-all-start = ((s32[64,1,32]{2,1,0:T(1,128)}), s32[64,1,32]{2,1,0:T(1,128)S(1)}, u32[]{:S(2)}, u32[]{:S(2)}) async-start(s32[64,1,32]{2,1,0:T(1,128)} %bitcast), calls=%async_computation | async-start | bytes 65536 | tf_op jit(solution)/shard_map/all_to_all | solution.py:71
  18.3 8.7 %scatter_custom_fusion.1 = f32[2048,768]{1,0:T(8,128)} fusion(s32[1024]{0:T(1024)S(1)} %get-tuple-element.9, f32[1024,768]{1,0:T(8,128)} %param.2, f32[]{:T(128)} %constant.39.clone.1), kind=kCustom, calls=%fused_computation.5 | custom fusion | bytes 6291968 | tf_op jit(solution)/shard_map/scatter | solution.py:61
  27.0 0.0 all-to-all-done
  27.0 10.5 %all-to-all-start.1 = ((f32[64,32,768]{2,1,0:T(8,128)}), f32[64,32,768]{2,1,0:T(8,128)}, u32[]{:S(2)}, u32[]{:S(2)}) async-start(f32[64,32,768]{2,1,0:T(8,128)} %bitcast.13), calls=%async_computation.1 | async-start | bytes 12582912 | tf_op jit(solution)/shard_map/all_to_all | solution.py:64
  37.5 0.5 broadcast.66
  38.0 0.7 reduce.8
  38.7 0.1 eq.62
  38.8 0.3 convert_reduce_fusion
  39.1 0.2 concatenate.12
  39.3 137.7 %all-to-all-done.1 = f32[64,32,768]{2,1,0:T(8,128)} async-done(((f32[64,32,768]{2,1,0:T(8,128)}), f32[64,32,768]{2,1,0:T(8,128)}, u32[]{:S(2)}, u32[]{:S(2)}) %all-to-all-start.1) | async-done | bytes 6291488 | tf_op jit(solution)/shard_map/all_to_all | solution.py:64
  177.0 3.3 %multiply_reduce_fusion = f32[64,32]{1,0:T(8,128)S(1)} fusion(f32[64,32,768]{2,1,0:T(8,128)} %all-to-all-done.1), kind=kLoop, calls=%fused_computation.2 | loop fusion | flops 3143680 | bytes 6299648 | tf_op jit(solution)/shard_map/reduce_sum | solution.py:84
  180.2 0.1 reshape.92
  180.3 6.2 %fusion.5 = f32[8,32,768]{2,1,0:T(8,128)S(1)} fusion(f32[2048,768,1]{1,0,2:T(8,128)} %bitcast.3, s32[2048]{0:T(1024)S(1)} %eq.62, s32[8,32]{1,0:T(8,128)S(1)} %multiply_add_fusion), kind=kOutput, calls=%fused_computation.9 | convolution fusion | flops 4832362496 | bytes 7087104 | tf_op jit(solution)/shard_map/dot_general | solution.py:78
  186.6 1.0 fusion.9
  187.6 0.1 pad_maximum_fusion
  187.7 37.4 %all_to_all.19 = f32[8,32,770]{2,1,0:T(8,128)S(1)} all-to-all(f32[8,32,770]{2,1,0:T(8,128)S(1)} %pad_maximum_fusion), channel_id=1, replica_groups=mesh['grp'=8,'dev'=64] {'grp'}, dimensions={0} | all-to-all | bytes 1576960 | tf_op jit(solution)/shard_map/all_to_all | solution.py:18
  225.2 0.1 reduce_sum.50
  225.2 0.1 fusion.18
  225.3 0.1 slice_divide_fusion
  225.5 0.1 copy.19
  225.5 0.1 fusion.17
  225.6 26.6 %all_gather.3 = f32[256,769]{1,0:T(8,128)S(1)} all-gather(f32[32,769]{1,0:T(8,128)S(1)} %pad_maximum_fusion.1), channel_id=1, replica_groups=mesh['grp'=8,'dev'=64] {'grp'}, dimensions={0}, use_global_device_ids=true | all-gather | bytes 885888 | tf_op jit(solution)/shard_map/all_gather | solution.py:35
  252.2 0.9 slice.8
  253.2 0.7 slice_reduce_fusion
  (2 shorter events, 0.0 us)
Async XLA Ops:
  7.6 19.3 %all-to-all-start = ((s32[64,1,32]{2,1,0:T(1,128)}), s32[64,1,32]{2,1,0:T(1,128)S(1)}, u32[]{:S(2)}, u32[]{:S(2)}) async-start(s32[64,1,32]{2,1,0:T(1,128)} %bitcast), calls=%async_computation | async-start | bytes 65536 | tf_op jit(solution)/shard_map/all_to_all | solution.py:71
  27.0 150.0 %all-to-all-start.1 = ((f32[64,32,768]{2,1,0:T(8,128)}), f32[64,32,768]{2,1,0:T(8,128)}, u32[]{:S(2)}, u32[]{:S(2)}) async-start(f32[64,32,768]{2,1,0:T(8,128)} %bitcast.13), calls=%async_computation.1 | async-start | bytes 12582912 | tf_op jit(solution)/shard_map/all_to_all | solution.py:64
where the time goes:
time: 254 us
  waiting for transfers between devices  138 us (54%)
  blocking collectives  64 us (25%)
  starting transfers between devices  21.2 us (8%)
  local copies, waits for them, and re-layouts  16.2 us (6%)
  matrix products  7.85 us (3%)
  other arithmetic  6.18 us (2%)
    all_to_all x1, waiting for transfers between devices, body(): lax.all_to_all(outgoing.reshape(owners, capacity, width), 'dev', split_ax...  138 us
    all_to_all x1, blocking collectives, sum_at_owner(): lax.all_to_all(parts, axis, split_axis=0, concat_axis=0, tiled=True)  37.4 us
    all_gather x1, blocking collectives, in_one_piece(): out, at, done = (lax.all_gather(both, axis, axis=dim, tiled=True), 0, [])  26.6 us
    all_to_all x1, starting transfers between devices, body(): lax.all_to_all(labels.reshape(owners, capacity), 'dev', split_axis=0, con...  10.7 us
    all_to_all x1, starting transfers between devices, body(): lax.all_to_all(outgoing.reshape(owners, capacity, width), 'dev', split_ax...  10.5 us
    scatter x1, local copies, waits for them, and re-layouts, body(): jnp.zeros((owners * capacity, width), jnp.float32).at[target].set(points)  8.66 us
    dot_general x1, matrix products, body(): jnp.dot(onehot, arrived, precision=lax.Precision.HIGHEST, preferred_eleme...  6.23 us
  transfers between devices with their start and end apart: 2, of which 1 were waited for; matrix products, arithmetic and copies ran while one was open for 4% of the time, Pallas kernels for 0%

commit v1 on v0

v1 whole, which is shorter than its diff:
```python
import jax
import jax.numpy as jnp
from jax import lax
from jax.experimental import pallas as pl
from jax.experimental.pallas import tpu as pltpu
from jax.sharding import Mesh
from jax.sharding import PartitionSpec as P

CL_OWN = 256
OWNERS = 64
LANES = 128
CAP = 32
MERGE = 32
PAIR = OWNERS // MERGE
SLOTS = PAIR * CAP
PARTS = 8
ROWS = CL_OWN // PARTS
SPREAD = PAIR * PARTS


def split3(value):
    first = value.astype(jnp.bfloat16)
    rest = value - first.astype(jnp.float32)
    second = rest.astype(jnp.bfloat16)
    third = (rest - second.astype(jnp.float32)).astype(jnp.bfloat16)
    return first, second, third


def pack_kernel(row_ref, left_ref, right_ref, aux_ref, out_ref):
    step = pl.program_id(0)
    last = pl.num_programs(0) - 1
    group = 2 * SLOTS

    @pl.when(step < last)
    def _():
        flat = out_ref.reshape(MERGE * group, LANES)

        def clear(g, carry):
            start = pl.multiple_of(g * group, 8)
            flat[pl.ds(start, group), :] = jnp.zeros((group, LANES), jnp.float32)
            return carry

        lax.fori_loop(0, MERGE, clear, 0)

        def place(i, carry):
            for r in range(8):
                at = row_ref[i * 8 + r]
                flat[pl.ds(at, 1), :] = left_ref[pl.ds(i * 8 + r, 1), :]
                flat[pl.ds(at + SLOTS, 1), :] = right_ref[pl.ds(i * 8 + r, 1), :]
            return carry

        lax.fori_loop(0, left_ref.shape[0] // 8, place, 0)

    @pl.when(step == last)
    def _():
        out_ref[:, :8, :] = aux_ref[...]


def pack(row, points, aux):
    rows, width = points.shape
    blocks = width // LANES
    steps = blocks // 2
    return pl.pallas_call(
        pack_kernel,
        grid=(steps + 1,),
        out_shape=jax.ShapeDtypeStruct((MERGE, blocks * SLOTS + 8, LANES), jnp.float32),
        in_specs=[
            pl.BlockSpec(memory_space=pltpu.SMEM),
            pl.BlockSpec((rows, LANES), lambda k: (0, 2 * jnp.minimum(k, steps - 1))),
            pl.BlockSpec((rows, LANES), lambda k: (0, 2 * jnp.minimum(k, steps - 1) + 1)),
            pl.BlockSpec(aux.shape, lambda k: (0, 0, 0)),
        ],
        out_specs=pl.BlockSpec((MERGE, 2 * SLOTS, LANES), lambda k: (0, k, 0)),
        compiler_params=pltpu.CompilerParams(vmem_limit_bytes=40 * 1024 * 1024),
        name="pack",
    )(row, points, points, aux)


def target_of(pair, part):
    return (2 * pair + part % 2) * 4 + part // 2


def merge_kernel(tags_ref, squares_ref, arrived_ref, out_ref, hot_ref):
    step = pl.program_id(0)
    tail = out_ref.shape[1] - 8

    @pl.when(step == 0)
    def _():
        cluster = lax.broadcasted_iota(jnp.int32, (CL_OWN, MERGE * CAP), 0) + 1
        for a in range(PAIR):
            tag = tags_ref[pl.ds(a, 1), :].astype(jnp.int32)
            hot = (cluster == tag).astype(jnp.float32).astype(jnp.bfloat16)
            hot_ref[a] = hot
            one, two, three = split3(squares_ref[pl.ds(a, 1), :])
            row = lax.broadcasted_iota(jnp.int32, (8, MERGE * CAP), 0)
            values = jnp.where(row == 0, 1.0, 0.0)
            values = jnp.where(row == 1, one.astype(jnp.float32), values)
            values = jnp.where(row == 2, two.astype(jnp.float32), values)
            values = jnp.where(row == 3, three.astype(jnp.float32), values)
            small = lax.dot_general(
                values.astype(jnp.bfloat16),
                hot,
                (((1,), (1,)), ((), ())),
                preferred_element_type=jnp.float32,
            )
            for part in range(PARTS):
                low = part * ROWS // LANES * LANES
                out_ref[target_of(a, part), tail:, :] = small[:, low : low + LANES]

    for a in range(PAIR):
        data = jnp.concatenate(
            [
                arrived_ref[:, j * SLOTS + a * CAP : j * SLOTS + (a + 1) * CAP, :].reshape(
                    MERGE * CAP, LANES
                )
                for j in range(2)
            ],
            axis=1,
        )
        hot = hot_ref[a]
        total = sum(
            jnp.dot(hot, term, preferred_element_type=jnp.float32)
            for term in reversed(split3(data))
        )
        for part in range(PARTS):
            for j in range(2):
                start = pl.multiple_of((2 * step + j) * ROWS, 8)
                out_ref[target_of(a, part), pl.ds(start, ROWS), :] = total[
                    part * ROWS : (part + 1) * ROWS, j * LANES : (j + 1) * LANES
                ]


def merge(tags, squares, arrived):
    blocks = (arrived.shape[1] - 8) // SLOTS
    shape = (SPREAD, blocks * ROWS + 8, LANES)
    return pl.pallas_call(
        merge_kernel,
        grid=(blocks // 2,),
        out_shape=jax.ShapeDtypeStruct(shape, jnp.float32),
        in_specs=[
            pl.BlockSpec(tags.shape, lambda k: (0, 0)),
            pl.BlockSpec(squares.shape, lambda k: (0, 0)),
            pl.BlockSpec((MERGE, 2 * SLOTS, LANES), lambda k: (0, k, 0)),
        ],
        out_specs=pl.BlockSpec(shape, lambda k: (0, 0, 0)),
        scratch_shapes=[pltpu.VMEM((PAIR, CL_OWN, MERGE * CAP), jnp.bfloat16)],
        compiler_params=pltpu.CompilerParams(vmem_limit_bytes=40 * 1024 * 1024),
        name="merge",
    )(tags, squares, arrived)


def finish_kernel(offset_ref, arrived_ref, out_ref):
    tail = out_ref.shape[0] - 8
    blocks = tail // ROWS
    total = arrived_ref[0]
    for k in range(1, SPREAD):
        total = total + arrived_ref[k]
    row = lax.broadcasted_iota(jnp.int32, (ROWS, LANES), 0)
    lane = lax.broadcasted_iota(jnp.int32, (ROWS, LANES), 1)
    mine = lane == row + offset_ref[0]
    squares = total[tail + 1 : tail + 2] + total[tail + 2 : tail + 3] + total[tail + 3 : tail + 4]
    counts = jnp.sum(jnp.where(mine, total[tail : tail + 1], 0.0), axis=1, keepdims=True)
    squares = jnp.sum(jnp.where(mine, squares, 0.0), axis=1, keepdims=True)
    denom = jnp.maximum(counts, 1.0)
    norm = jnp.zeros((ROWS, LANES), jnp.float32)
    for j in range(blocks):
        sums = total[j * ROWS : (j + 1) * ROWS]
        norm = norm + sums * sums
        out_ref[j * ROWS : (j + 1) * ROWS, :] = sums / denom
    norm = jnp.sum(norm, axis=1, keepdims=True)
    spread = (squares - norm / denom) / (denom * (blocks * LANES))
    flat = jnp.sum(jnp.where(lane == row, spread, 0.0), axis=0, keepdims=True)
    out_ref[tail:, :] = jnp.broadcast_to(flat, (8, LANES))


def finish(offset, arrived):
    return pl.pallas_call(
        finish_kernel,
        out_shape=jax.ShapeDtypeStruct(arrived.shape[1:], jnp.float32),
        in_specs=[
            pl.BlockSpec(memory_space=pltpu.SMEM),
            pl.BlockSpec(memory_space=pltpu.VMEM),
        ],
        out_specs=pl.BlockSpec(memory_space=pltpu.VMEM),
        name="finish",
    )(offset, arrived)


def body(points, assignment):
    rows, width = points.shape
    blocks = width // LANES
    owner = assignment >> 8
    label = assignment & (CL_OWN - 1)
    slot = ((owner >> 4) * 8 + (owner & 7)) * 2 + ((owner >> 3) & 1)
    matches = slot[:, None] == jnp.arange(OWNERS, dtype=jnp.int32)[None, :]
    matches = matches.astype(jnp.float32)
    earlier = (jnp.arange(rows)[:, None] > jnp.arange(rows)[None, :]).astype(jnp.float32)
    before = jnp.dot(earlier, matches, preferred_element_type=jnp.float32)
    position = jnp.sum(before * matches, axis=1).astype(jnp.int32)
    row = (slot >> 1) * (2 * SLOTS) + (slot & 1) * CAP + position
    at = (position[:, None] == jnp.arange(CAP, dtype=jnp.int32)[None, :]).astype(jnp.float32)
    norms = jnp.sum(points * points, axis=1)
    values = jnp.concatenate(
        [at * (label + 1).astype(jnp.float32)[:, None], at * norms[:, None]], axis=1
    )
    placed = lax.dot_general(
        matches,
        values,
        (((0,), (0,)), ((), ())),
        precision=lax.Precision.HIGHEST,
        preferred_element_type=jnp.float32,
    )
    aux = placed.reshape(MERGE, PAIR, 2, CAP).transpose(0, 2, 1, 3).reshape(MERGE, 2, SLOTS)
    aux = jnp.pad(aux, ((0, 0), (0, 6), (0, LANES - SLOTS)))

    outgoing = pack(row, points, aux)
    arrived = lax.all_to_all(
        outgoing, ("x", "zb", "yb", "c"), split_axis=0, concat_axis=0, tiled=True
    )
    info = arrived[:, blocks * SLOTS : blocks * SLOTS + 2, :SLOTS]
    info = info.reshape(MERGE, 2, PAIR, CAP).transpose(1, 2, 0, 3).reshape(2, PAIR, MERGE * CAP)

    partial = merge(info[0], info[1], arrived)
    arrived = lax.all_to_all(partial, ("yp", "zp"), split_axis=0, concat_axis=0, tiled=True)

    part = 2 * lax.axis_index("zp") + lax.axis_index("yp") % 2
    offset = (part * ROWS % LANES).astype(jnp.int32).reshape(1)
    done = finish(offset, arrived)
    moves = []
    for zb in range(2):
        for yp in range(4):
            here = zb * 4 + yp
            moves.append((here, here if yp % 2 == zb else (zb ^ 1) * 4 + (yp ^ 1)))
    done = lax.ppermute(done, ("zb", "yp"), moves)
    whole = lax.all_gather(done, ("zp", "zb"), axis=0, tiled=False)
    centre = whole[:, : blocks * ROWS].reshape(PARTS, blocks, ROWS, LANES)
    centre = centre.transpose(0, 2, 1, 3).reshape(CL_OWN, width)
    spread = whole[:, blocks * ROWS, :ROWS].reshape(CL_OWN)
    return centre, spread


def solution(mesh):
    fine = Mesh(
        mesh.devices.reshape(4, 2, 4, 4, 2, 2), ("zp", "zb", "x", "yp", "yb", "c")
    )
    every = ("zp", "zb", "x", "yp", "yb", "c")
    owners = ("x", "yp", "yb", "c")
    return jax.shard_map(
        body,
        mesh=fine,
        in_specs=(P(every, None), P(every)),
        out_specs=(P(owners, None), P(owners)),
        check_vma=False,
    )
```

time: 254 us -> 208 us (0.82)
  the two profiles are of different devices: /device:TPU:2 before, /device:TPU:42 now
where the time goes in v1:
time: 208 us
  blocking collectives  117 us (56%)
  waiting for transfers between devices  44.8 us (22%)
  starting transfers between devices  16.3 us (8%)
  Pallas kernels  14.1 us (7%)
  local copies, waits for them, and re-layouts  9.48 us (5%)
  other arithmetic  4.27 us (2%)
    all_to_all x1, blocking collectives, body(): lax.all_to_all(outgoing, ('x', 'zb', 'yb', 'c'), split_axis=0, concat_axi...  79.9 us
    all_to_all x1, waiting for transfers between devices, body(): lax.all_to_all(partial, ('yp', 'zp'), split_axis=0, concat_axis=0, tiled=...  44.8 us
    all_gather x1, blocking collectives, body(): whole = lax.all_gather(done, ('zp', 'zb'), axis=0, tiled=False)  37.4 us
    all_to_all x1, starting transfers between devices, body(): lax.all_to_all(partial, ('yp', 'zp'), split_axis=0, concat_axis=0, tiled=...  14.8 us
    unnamed x9, local copies, waits for them, and re-layouts  7.72 us
    pallas_call x1, Pallas kernels, pack(): pl.pallas_call(pack_kernel, grid=(steps + 1,), out_shape=jax.ShapeDtypeSt...  6.49 us
    pallas_call x1, Pallas kernels, merge(): pl.pallas_call(merge_kernel, grid=(blocks // 2,), out_shape=jax.ShapeDtyp...  5.41 us
  transfers between devices with their start and end apart: 2, of which 1 were waited for; matrix products, arithmetic and copies ran while one was open for 0% of the time, Pallas kernels for 0%

profile of v1, /device:TPU:42, one launch (start us, length us, event | category | flops | bytes accessed | tf_op | source)
XLA Modules:
  0.0 208.1 jit_solution(14677569230240372062)
XLA Ops:
  0.6 0.7 and_add_fusion
  1.3 0.6 fusion.2
  1.9 0.0 copy-start
  2.0 0.9 add_convert_fusion
  2.8 2.3 %multiply_reduce_fusion = f32[1024]{0:T(1024)S(1)} fusion(f32[1024,768]{1,0:T(8,128)} %right_ref.1), kind=kLoop, calls=%fused_computation.2 | loop fusion | flops 1571840 | bytes 3149824 | tf_op jit(solution)/shard_map/reduce_sum | solution.py:202
  5.1 0.5 fusion.8
  5.5 0.4 fusion.3
  6.0 0.1 reshape.34
  6.1 0.1 reshape.35
  6.3 0.0 copy-done
  6.3 6.5 %pack.1 = f32[32,392,128]{2,1,0:T(8,128)S(1)} custom-call(s32[1024]{0:T(1024)S(1)} %get-tuple-element.7.row_ref, f32[1024,768]{1,0:T(8,128)S(1)} %copy-done, f32[1024,768]{1,0:T(8,128)S(1)} %copy-done, f32[32,8,128]{2,1,0:T(8,128)S(1)} %pad.4.aux_ref), custom_call_target="tpu_custom_call" | custom-call | tf_op jit(solution)/shard_map/pack/pallas_call | solution.py:63
  12.8 79.9 %all_to_all.10.arrived_ref = f32[32,392,128]{2,1,0:T(8,128)S(1)} all-to-all(f32[32,392,128]{2,1,0:T(8,128)S(1)} %pack.1), channel_id=1, replica_groups=mesh['zp'=4,'zb'=2,'x'=4,'yp'=4,'yb'=2,'c'=2] {'x','zb','yb','c'}, dimensions={0} | all-to-all | bytes 12845056 | tf_op jit(solution)/shard_map/all_to_all | solution.py:217
  92.7 0.0 copy-start.1
  92.7 2.7 %copy-done.1 = f32[32,392,128]{2,1,0:T(8,128)} copy-done((f32[32,392,128]{2,1,0:T(8,128)}, f32[32,392,128]{2,1,0:T(8,128)S(1)}, u32[]{:S(2)}) %copy-start.1) | copy-done | bytes 6422552
  95.4 0.1 reshape.36
  95.5 0.1 squeeze.7.squares_ref
  95.6 0.1 squeeze.6.tags_ref
  95.7 0.0 copy-start.2
  95.7 2.8 %copy-done.2 = f32[32,392,128]{2,1,0:T(8,128)S(1)} copy-done((f32[32,392,128]{2,1,0:T(8,128)S(1)}, f32[32,392,128]{2,1,0:T(8,128)}, u32[]{:S(2)}) %copy-start.2) | copy-done | bytes 6422552
  98.6 5.4 %merge.1 = f32[16,200,128]{2,1,0:T(8,128)} custom-call(f32[2,1024]{1,0:T(2,128)S(1)} %squeeze.6.tags_ref, f32[2,1024]{1,0:T(2,128)S(1)} %squeeze.7.squares_ref, f32[32,392,128]{2,1,0:T(8,128)S(1)} %copy-done.2), custom_call_target="tpu_custom_call" | custom-call | tf_op jit(solution)/shard_map/merge/pallas_call | solution.py:136
  104.0 14.8 %all-to-all-start.1 = ((f32[16,200,128]{2,1,0:T(8,128)}), f32[16,200,128]{2,1,0:T(8,128)S(1)}, u32[]{:S(2)}, u32[]{:S(2)}) async-start(f32[16,200,128]{2,1,0:T(8,128)} %merge.1), calls=%async_computation.1 | async-start | bytes 3276800 | tf_op jit(solution)/shard_map/all_to_all | solution.py:224
  118.8 44.8 %all-to-all-done.1.arrived_ref = f32[16,200,128]{2,1,0:T(8,128)S(1)} async-done(((f32[16,200,128]{2,1,0:T(8,128)}), f32[16,200,128]{2,1,0:T(8,128)S(1)}, u32[]{:S(2)}, u32[]{:S(2)}) %all-to-all-start.1) | async-done | bytes 1638432 | tf_op jit(solution)/shard_map/all_to_all | solution.py:224
  163.5 0.0 copy-start.3
  163.5 1.2 copy-done.3
  164.7 2.2 %finish.1 = f32[200,128]{1,0:T(8,128)} custom-call(s32[1]{0:T(128)} %bitcast.offset_ref, f32[16,200,128]{2,1,0:T(8,128)} %copy-done.3), custom_call_target="tpu_custom_call" | custom-call | tf_op jit(solution)/shard_map/finish/pallas_call | solution.py:177
  167.0 1.5 collective-permute-start
  168.5 0.0 collective-permute-done
  168.5 37.4 %all-gather = f32[1600,128]{1,0:T(8,128)S(1)} all-gather(f32[200,128]{1,0:T(8,128)S(1)} %collective-permute-done), channel_id=2, replica_groups=mesh['zp'=4,'zb'=2,'x'=4,'yp'=4,'yb'=2,'c'=2] {'zp','zb'}, dimensions={0}, use_global_device_ids=true | all-gather | bytes 921600 | tf_op jit(solution)/shard_map/all_gather | solution.py:235
  205.9 0.1 slice.25
  206.0 0.6 reshape_squeeze.3
  206.6 0.5 copy.14
  207.1 1.0 copy.18
  (8 shorter events, 0.1 us)
Async XLA Ops:
  1.9 4.3 %copy-start = (f32[1024,768]{1,0:T(8,128)S(1)}, f32[1024,768]{1,0:T(8,128)}, u32[]{:S(2)}) copy-start(f32[1024,768]{1,0:T(8,128)} %right_ref.1) | copy-start | bytes 9437188
  92.7 2.7 %copy-start.1 = (f32[32,392,128]{2,1,0:T(8,128)}, f32[32,392,128]{2,1,0:T(8,128)S(1)}, u32[]{:S(2)}) copy-start(f32[32,392,128]{2,1,0:T(8,128)S(1)} %all_to_all.10.arrived_ref) | copy-start | bytes 19267588
  95.7 2.8 %copy-start.2 = (f32[32,392,128]{2,1,0:T(8,128)S(1)}, f32[32,392,128]{2,1,0:T(8,128)}, u32[]{:S(2)}) copy-start(f32[32,392,128]{2,1,0:T(8,128)} %copy-done.1) | copy-start | bytes 19267588
  104.0 59.6 %all-to-all-start.1 = ((f32[16,200,128]{2,1,0:T(8,128)}), f32[16,200,128]{2,1,0:T(8,128)S(1)}, u32[]{:S(2)}, u32[]{:S(2)}) async-start(f32[16,200,128]{2,1,0:T(8,128)} %merge.1), calls=%async_computation.1 | async-start | bytes 3276800 | tf_op jit(solution)/shard_map/all_to_all | solution.py:224
  163.5 1.2 copy-start.3
  167.0 1.5 collective-permute-start

commit v2 on v0

v2 whole, which is shorter than its diff:
```python
import jax
import jax.numpy as jnp
from jax import lax
from jax.experimental import pallas as pl
from jax.experimental.pallas import tpu as pltpu
from jax.sharding import Mesh
from jax.sharding import PartitionSpec as P

CL_OWN = 256
OWNERS = 64
LANES = 128
CAP = 32
MERGE = 32
PAIR = OWNERS // MERGE
SLOTS = PAIR * CAP
PARTS = 8
ROWS = CL_OWN // PARTS
SIDE = 4
KEYS = MERGE * CAP
GATHER = LANES // CAP
TAIL = 8


def split3(value):
    first = value.astype(jnp.bfloat16)
    rest = value - first.astype(jnp.float32)
    second = rest.astype(jnp.bfloat16)
    third = (rest - second.astype(jnp.float32)).astype(jnp.bfloat16)
    return first, second, third


def whole(space=pltpu.VMEM):
    return pl.BlockSpec(memory_space=space)


def params():
    return pltpu.CompilerParams(vmem_limit_bytes=48 * 1024 * 1024)


def pack_kernel(row_ref, *refs):
    *block_refs, aux_ref, out_ref = refs
    blocks = len(block_refs)
    stride = blocks * SLOTS + TAIL
    flat = out_ref.reshape(MERGE * stride, LANES)

    def clear(g, carry):
        start = pl.multiple_of(g * stride, 8)
        flat[pl.ds(start, stride - TAIL), :] = jnp.zeros((stride - TAIL, LANES), jnp.float32)
        flat[pl.ds(start + stride - TAIL, TAIL), :] = aux_ref[g]
        return carry

    lax.fori_loop(0, MERGE, clear, 0)

    def place(i, carry):
        for r in range(8):
            at = row_ref[i * 8 + r]
            for j, ref in enumerate(block_refs):
                flat[pl.ds(at + j * SLOTS, 1), :] = ref[pl.ds(i * 8 + r, 1), :]
        return carry

    lax.fori_loop(0, block_refs[0].shape[0] // 8, place, 0)


def pack(row, points, aux, first, blocks):
    rows = points.shape[0]

    def column(j):
        return pl.BlockSpec((rows, LANES), lambda i: (0, j))

    shape = (MERGE, blocks * SLOTS + TAIL, LANES)
    return pl.pallas_call(
        pack_kernel,
        grid=(1,),
        out_shape=jax.ShapeDtypeStruct(shape, jnp.float32),
        in_specs=[
            pl.BlockSpec(memory_space=pltpu.SMEM),
            *[column(first + j) for j in range(blocks)],
            pl.BlockSpec(aux.shape, lambda i: (0, 0, 0)),
        ],
        out_specs=pl.BlockSpec(shape, lambda i: (0, 0, 0)),
        compiler_params=params(),
        name="pack",
    )(row, *[points] * blocks, aux)


def lane_rows(arrived_ref):
    tail = arrived_ref.shape[1] - TAIL
    tiles = []
    for k in range(MERGE // GATHER):
        tile = arrived_ref[k * GATHER, tail:, :]
        for s in range(1, GATHER):
            tile = tile + arrived_ref[k * GATHER + s, tail:, :]
        tiles.append(tile)
    return jnp.concatenate(tiles, axis=1)


def one_hot(tags):
    cluster = lax.broadcasted_iota(jnp.int32, (CL_OWN, KEYS), 0) + 1
    return (cluster == tags.astype(jnp.int32)).astype(jnp.float32).astype(jnp.bfloat16)


def owner_sums(hot, arrived_ref, a):
    blocks = (arrived_ref.shape[1] - TAIL) // SLOTS
    terms = []
    for j in range(blocks):
        low = j * SLOTS + a * CAP
        terms.append(split3(arrived_ref[:, low : low + CAP, :].reshape(KEYS, LANES)))
    columns = jnp.concatenate([t[k] for k in range(3) for t in terms], axis=1)
    total = jnp.dot(hot, columns, preferred_element_type=jnp.float32)
    wide = blocks * LANES
    return total[:, 2 * wide :] + total[:, wide : 2 * wide] + total[:, :wide]


def row_sums(hot, rows):
    return lax.dot_general(
        rows.astype(jnp.bfloat16), hot, (((1,), (1,)), ((), ())), preferred_element_type=jnp.float32
    )


def merge_a_kernel(side_ref, arrived_ref, tags_ref, *refs):
    *out_refs, sums_ref, small_ref = refs
    blocks = (arrived_ref.shape[1] - TAIL) // SLOTS
    tags = lane_rows(arrived_ref)
    tags_ref[...] = tags
    for a in range(PAIR):
        hot = one_hot(tags[a : a + 1])
        row = lax.broadcasted_iota(jnp.int32, (TAIL, KEYS), 0)
        small_ref[a] = row_sums(hot, jnp.where(row == 0, 1.0, 0.0))
        sums_ref[a] = owner_sums(hot, arrived_ref, a)
    for k in range(SIDE):
        there = (side_ref[0] + k) & (SIDE - 1)
        a = there >> 1
        odd = there & 1
        for zp in range(SIDE):
            low = pl.multiple_of((2 * zp + odd) * ROWS, ROWS)
            sums = sums_ref[a, pl.ds(low, ROWS), :]
            for j in range(blocks):
                out_refs[k][zp, j * ROWS : (j + 1) * ROWS, :] = sums[
                    :, j * LANES : (j + 1) * LANES
                ]
            half = 2 * zp * ROWS // LANES * LANES
            out_refs[k][zp, blocks * ROWS :, :] = small_ref[a, :, half : half + LANES]


def merge_a(side, arrived):
    blocks = (arrived.shape[1] - TAIL) // SLOTS
    part = jax.ShapeDtypeStruct((SIDE, blocks * ROWS + TAIL, LANES), jnp.float32)
    return pl.pallas_call(
        merge_a_kernel,
        out_shape=[jax.ShapeDtypeStruct((TAIL, KEYS), jnp.float32), *[part] * SIDE],
        in_specs=[whole(pltpu.SMEM), whole()],
        out_specs=[whole()] * (SIDE + 1),
        scratch_shapes=[
            pltpu.VMEM((PAIR, CL_OWN, blocks * LANES), jnp.float32),
            pltpu.VMEM((PAIR, TAIL, CL_OWN), jnp.float32),
        ],
        compiler_params=params(),
        name="merge_a",
    )(side, arrived)


def merge_b_kernel(tags_ref, arrived_ref, after_ref, out_ref):
    blocks = (arrived_ref.shape[1] - TAIL) // SLOTS
    norms = lane_rows(arrived_ref)
    for a in range(PAIR):
        hot = one_hot(tags_ref[a : a + 1, :])
        one, two, three = split3(norms[a : a + 1])
        row = lax.broadcasted_iota(jnp.int32, (TAIL, KEYS), 0)
        values = jnp.where(row == 0, one.astype(jnp.float32), 0.0)
        values = jnp.where(row == 1, two.astype(jnp.float32), values)
        values = jnp.where(row == 2, three.astype(jnp.float32), values)
        small = row_sums(hot, values)
        total = owner_sums(hot, arrived_ref, a)
        for part in range(PARTS):
            target = (2 * a + part % 2) * SIDE + part // 2
            for j in range(blocks):
                out_ref[target, j * ROWS : (j + 1) * ROWS, :] = total[
                    part * ROWS : (part + 1) * ROWS, j * LANES : (j + 1) * LANES
                ]
            half = part * ROWS // LANES * LANES
            out_ref[target, blocks * ROWS :, :] = small[:, half : half + LANES]


def merge_b(tags, arrived, after):
    blocks = (arrived.shape[1] - TAIL) // SLOTS
    shape = (SIDE * SIDE, blocks * ROWS + TAIL, LANES)
    return pl.pallas_call(
        merge_b_kernel,
        out_shape=jax.ShapeDtypeStruct(shape, jnp.float32),
        in_specs=[whole(), whole(), whole(pl.ANY)],
        out_specs=whole(),
        compiler_params=params(),
        name="merge_b",
    )(tags, arrived, after)


def add_kernel(side_ref, own_ref, *refs):
    *in_refs, sums_ref = refs[: SIDE - 1] + refs[-1:]
    out_refs = refs[SIDE - 1 : -1]
    sums_ref[...] = own_ref[...] + in_refs[0][...] + in_refs[1][...] + in_refs[2][...]
    for k in range(SIDE):
        out_refs[k][...] = sums_ref[(side_ref[0] + k) & (SIDE - 1)]


def add(side, own, others):
    part = jax.ShapeDtypeStruct(own.shape[1:], jnp.float32)
    return pl.pallas_call(
        add_kernel,
        out_shape=[part] * SIDE,
        in_specs=[whole(pltpu.SMEM)] + [whole()] * SIDE,
        out_specs=[whole()] * SIDE,
        scratch_shapes=[pltpu.VMEM(own.shape, jnp.float32)],
        compiler_params=params(),
        name="add",
    )(side, own, *others)


def column_of(row, offset):
    at = lax.broadcasted_iota(jnp.int32, (ROWS, LANES), 0) + offset
    lane = lax.broadcasted_iota(jnp.int32, (ROWS, LANES), 1)
    return jnp.sum(jnp.where(lane == at, row, 0.0), axis=1, keepdims=True)


def finish_a_kernel(offset_ref, own_ref, one_ref, two_ref, three_ref, out_ref, denom_ref, norm_ref):
    total = own_ref[...] + one_ref[...] + two_ref[...] + three_ref[...]
    tail = total.shape[0] - TAIL
    denom = jnp.maximum(column_of(total[tail : tail + 1], offset_ref[0]), 1.0)
    norm = jnp.zeros((ROWS, LANES), jnp.float32)
    for low in range(0, tail, ROWS):
        sums = total[low : low + ROWS]
        norm = norm + sums * sums
        out_ref[low : low + ROWS, :] = sums / denom
    denom_ref[...] = jnp.broadcast_to(denom, (ROWS, LANES))
    norm_ref[...] = norm


def finish_a(offset, own, others):
    tile = jax.ShapeDtypeStruct((ROWS, LANES), jnp.float32)
    return pl.pallas_call(
        finish_a_kernel,
        out_shape=[
            jax.ShapeDtypeStruct((own.shape[0] - TAIL, LANES), jnp.float32),
            tile,
            tile,
        ],
        in_specs=[whole(pltpu.SMEM)] + [whole()] * SIDE,
        out_specs=[whole()] * 3,
        compiler_params=params(),
        name="finish_a",
    )(offset, own, *others)


def finish_b_kernel(width, offset_ref, arrived_ref, denom_ref, norm_ref, after_ref, out_ref):
    total = arrived_ref[0]
    for k in range(1, SIDE * SIDE):
        total = total + arrived_ref[k]
    tail = total.shape[0] - TAIL
    squares = total[tail : tail + 1] + total[tail + 1 : tail + 2] + total[tail + 2 : tail + 3]
    squares = column_of(squares, offset_ref[0])
    denom = denom_ref[:, :1]
    norm = norm_ref[...]
    for low in range(0, tail, ROWS):
        sums = total[low : low + ROWS]
        norm = norm + sums * sums
        out_ref[low : low + ROWS, :] = sums / denom
    norm = jnp.sum(norm, axis=1, keepdims=True)
    spread = (squares - norm / denom) / (denom * width)
    row = lax.broadcasted_iota(jnp.int32, (ROWS, LANES), 0)
    lane = lax.broadcasted_iota(jnp.int32, (ROWS, LANES), 1)
    flat = jnp.sum(jnp.where(lane == row, spread, 0.0), axis=0, keepdims=True)
    out_ref[tail:, :] = jnp.broadcast_to(flat, (TAIL, LANES))


def finish_b(width, offset, arrived, denom, norm, after):
    return pl.pallas_call(
        lambda *refs: finish_b_kernel(width, *refs),
        out_shape=jax.ShapeDtypeStruct(arrived.shape[1:], jnp.float32),
        in_specs=[whole(pltpu.SMEM)] + [whole()] * 3 + [whole(pl.ANY)],
        out_specs=whole(),
        compiler_params=params(),
        name="finish_b",
    )(offset, arrived, denom, norm, after)


def lay_kernel(a_ref, b_ref, out_ref):
    blocks = out_ref.shape[1] // LANES
    left = a_ref.shape[1] // ROWS
    for part in range(PARTS):
        for j in range(blocks):
            ref, at = (a_ref, j) if j < left else (b_ref, j - left)
            out_ref[part * ROWS : (part + 1) * ROWS, j * LANES : (j + 1) * LANES] = ref[
                part, at * ROWS : (at + 1) * ROWS, :
            ]


def lay(a, b, width):
    return pl.pallas_call(
        lay_kernel,
        out_shape=jax.ShapeDtypeStruct((CL_OWN, width), jnp.float32),
        in_specs=[whole(), whole()],
        out_specs=whole(),
        compiler_params=params(),
        name="lay",
    )(a, b)


def shifted(parts, axis):
    return [
        lax.ppermute(part, axis, [(j, (j + k) % SIDE) for j in range(SIDE)])
        for k, part in enumerate(parts, 1)
    ]


def to_owner(value):
    moves = []
    for zb in range(2):
        for yp in range(SIDE):
            here = zb * SIDE + yp
            moves.append((here, here if yp % 2 == zb else (zb ^ 1) * SIDE + (yp ^ 1)))
    value = lax.ppermute(value, ("zb", "yp"), moves)
    return lax.all_gather(value, ("zp", "zb"), axis=0, tiled=False)


def meet(value):
    return lax.all_to_all(value, ("x", "zb", "yb", "c"), split_axis=0, concat_axis=0, tiled=True)


def body(points, assignment):
    rows, width = points.shape
    blocks = width // LANES
    left = blocks // 2
    owner = assignment >> 8
    label = assignment & (CL_OWN - 1)
    slot = ((owner >> 4) * 8 + (owner & 7)) * 2 + ((owner >> 3) & 1)
    matches = slot[:, None] == jnp.arange(OWNERS, dtype=jnp.int32)[None, :]
    matches = matches.astype(jnp.float32)
    earlier = (jnp.arange(rows)[:, None] > jnp.arange(rows)[None, :]).astype(jnp.float32)
    before = jnp.dot(earlier, matches, preferred_element_type=jnp.float32)
    position = jnp.sum(before * matches, axis=1).astype(jnp.int32)
    inside = (slot & 1) * CAP + position
    row_a = (slot >> 1) * (left * SLOTS + TAIL) + inside
    row_b = (slot >> 1) * ((blocks - left) * SLOTS + TAIL) + inside
    place = position[:, None] == jnp.arange(CAP, dtype=jnp.int32)[None, :]
    group = (lax.axis_index("yb") * 2 + lax.axis_index("c")) % GATHER
    lanes = jnp.arange(LANES, dtype=jnp.int32)[None, None, :] // CAP == group

    def tails(value, precision):
        at = jnp.where(place, value[:, None], 0.0)
        placed = lax.dot_general(
            matches,
            at,
            (((0,), (0,)), ((), ())),
            precision=precision,
            preferred_element_type=jnp.float32,
        )
        placed = jnp.tile(placed.reshape(MERGE, PAIR, CAP), (1, 1, GATHER))
        return jnp.pad(jnp.where(lanes, placed, 0.0), ((0, 0), (0, TAIL - PAIR), (0, 0)))

    yp = lax.axis_index("yp")
    zp = lax.axis_index("zp")
    offset = ((2 * zp + (yp & 1)) * ROWS % LANES).reshape(1)

    tags = tails((label + 1).astype(jnp.float32), lax.Precision.DEFAULT)
    packed = pack(row_a, points, tags, 0, left)
    met_a = meet(packed)
    later, _ = lax.optimization_barrier((points, packed))
    norms = tails(jnp.sum(later * later, axis=1), lax.Precision.HIGHEST)
    met_b = meet(pack(row_b, points, norms, left, blocks - left))

    tags, own, *rest = merge_a(yp.reshape(1), met_a)
    own, *rest = add(zp.reshape(1), own, shifted(rest, "yp"))
    done_a, denom, norm = finish_a(offset, own, shifted(rest, "zp"))
    all_a = to_owner(done_a)

    partial = merge_b(tags, met_b, denom)
    partial = lax.all_to_all(partial, ("yp", "zp"), split_axis=0, concat_axis=0, tiled=True)
    all_b = to_owner(finish_b(width, offset, partial, denom, norm, all_a))
    centre = lay(all_a, all_b, width)
    spread = all_b[:, -TAIL, :ROWS].reshape(CL_OWN)
    return centre, spread


def solution(mesh):
    fine = Mesh(mesh.devices.reshape(4, 2, 4, 4, 2, 2), ("zp", "zb", "x", "yp", "yb", "c"))
    every = ("zp", "zb", "x", "yp", "yb", "c")
    owners = ("x", "yp", "yb", "c")
    return jax.shard_map(
        body,
        mesh=fine,
        in_specs=(P(every, None), P(every)),
        out_specs=(P(owners, None), P(owners)),
        check_vma=False,
    )
```

time: 254 us -> 244 us (0.961)
  the two profiles are of different devices: /device:TPU:2 before, /device:TPU:18 now
where the time goes in v2:
time: 244 us
  waiting for transfers between devices  96.4 us (40%)
  starting transfers between devices  61.5 us (25%)
  blocking collectives  57.1 us (23%)
  Pallas kernels  18.6 us (8%)
  local copies, waits for them, and re-layouts  5.76 us (2%)
    all_gather x2, blocking collectives, to_owner(): return lax.all_gather(value, ('zp', 'zb'), axis=0, tiled=False)  57.1 us
    ppermute x6, waiting for transfers between devices, shifted(): lax.ppermute(part, axis, [(j, (j + k) % SIDE) for j in range(SIDE)])  41.6 us
    ppermute x6, starting transfers between devices, shifted(): lax.ppermute(part, axis, [(j, (j + k) % SIDE) for j in range(SIDE)])  33.5 us
    all_to_all x2, waiting for transfers between devices, meet(): lax.all_to_all(value, ('x', 'zb', 'yb', 'c'), split_axis=0, concat_axis=0...  33.4 us
    ppermute x2, waiting for transfers between devices, to_owner(): value = lax.ppermute(value, ('zb', 'yp'), moves)  21.4 us
    all_to_all x2, starting transfers between devices, meet(): lax.all_to_all(value, ('x', 'zb', 'yb', 'c'), split_axis=0, concat_axis=0...  14.9 us
    pallas_call x2, Pallas kernels, pack(): pl.pallas_call(pack_kernel, grid=(1,), out_shape=jax.ShapeDtypeStruct(sha...  9.09 us
    all_to_all x1, starting transfers between devices, body(): lax.all_to_all(partial, ('yp', 'zp'), split_axis=0, concat_axis=0, tiled=...  7.23 us
  transfers between devices with their start and end apart: 11, of which 6 were waited for; matrix products, arithmetic and copies ran while one was open for 0% of the time, Pallas kernels for 5%

profile of v2, /device:TPU:18, one launch (start us, length us, event | category | flops | bytes accessed | tf_op | source)
XLA Modules:
  0.0 243.6 jit_solution(17914935122168390686)
XLA Ops:
  0.6 0.7 and_add_fusion
  1.3 0.6 fusion.2
  2.0 0.7 add_convert_fusion
  2.7 0.5 fusion.5
  3.2 0.1 tile.22
  3.3 0.0 copy-start
  3.4 1.9 copy-done
  5.2 4.6 %pack.2 = f32[32,200,128]{2,1,0:T(8,128)} custom-call(s32[1024]{0:T(1024)S(1)} %get-tuple-element.29.row_ref, f32[1024,768]{1,0:T(8,128)S(1)} %copy-done, f32[1024,768]{1,0:T(8,128)S(1)} %copy-done, f32[1024,768]{1,0:T(8,128)S(1)} %copy-done, f32[32,8,128]{2,1,0:T(8,128)S(1)} %pad.7.refs_3_), custom_call_target="tpu_custom_call" | custom-call | tf_op jit(solution)/shard_map/pack/pallas_call | solution.py:71
  9.8 0.0 copy-start.1
  9.8 8.1 %all-to-all-start = ((f32[32,200,128]{2,1,0:T(8,128)}), f32[32,200,128]{2,1,0:T(8,128)}, u32[]{:S(2)}, u32[]{:S(2)}) async-start(f32[32,200,128]{2,1,0:T(8,128)} %pack.2), calls=%async_computation | async-start | bytes 6553600 | tf_op jit(solution)/shard_map/all_to_all | solution.py:325
  17.9 0.0 copy-done.1
  18.0 0.3 multiply_reduce_fusion
  18.2 0.5 fusion.3
  18.8 0.1 tile.25
  19.0 4.5 %pack.3 = f32[32,200,128]{2,1,0:T(8,128)} custom-call(s32[1024]{0:T(1024)S(1)} %get-tuple-element.29.row_ref, f32[1024,768]{1,0:T(8,128)S(1)} %copy-done.1, f32[1024,768]{1,0:T(8,128)S(1)} %copy-done.1, f32[1024,768]{1,0:T(8,128)S(1)} %copy-done.1, f32[32,8,128]{2,1,0:T(8,128)S(1)} %pad.8.refs_3_), custom_call_target="tpu_custom_call" | custom-call | tf_op jit(solution)/shard_map/pack/pallas_call | solution.py:71
  23.5 33.4 %all-to-all-done.arrived_ref = f32[32,200,128]{2,1,0:T(8,128)} async-done(((f32[32,200,128]{2,1,0:T(8,128)}), f32[32,200,128]{2,1,0:T(8,128)}, u32[]{:S(2)}, u32[]{:S(2)}) %all-to-all-start) | async-done | bytes 3276832 | tf_op jit(solution)/shard_map/all_to_all | solution.py:325
  56.9 6.8 %all-to-all-start.1 = ((f32[32,200,128]{2,1,0:T(8,128)}), f32[32,200,128]{2,1,0:T(8,128)S(1)}, u32[]{:S(2)}, u32[]{:S(2)}) async-start(f32[32,200,128]{2,1,0:T(8,128)} %pack.3), calls=%async_computation.1 | async-start | bytes 6553600 | tf_op jit(solution)/shard_map/all_to_all | solution.py:325
  63.7 4.7 %merge_a.1 = (f32[8,1024]{1,0:T(8,128)S(1)}, f32[4,104,128]{2,1,0:T(8,128)S(1)}, f32[4,104,128]{2,1,0:T(8,128)}, f32[4,104,128]{2,1,0:T(8,128)}, f32[4,104,128]{2,1,0:T(8,128)}) custom-call(s32[1]{0:T(128)} %bitcast.2.side_ref, f32[32,200,128]{2,1,0:T(8,128)} %all-to-all-done.arrived_ref), custom_call_target="tpu_custom_call" | custom-call | tf_op jit(solution)/shard_map/merge_a/pallas_call | solution.py:148
  68.4 0.0 copy-start.3
  68.4 0.6 copy-done.3
  69.0 4.8 %collective-permute-start = (f32[4,104,128]{2,1,0:T(8,128)}, f32[4,104,128]{2,1,0:T(8,128)}, u32[]{:S(2)}, u32[]{:S(2)}) collective-permute-start(f32[4,104,128]{2,1,0:T(8,128)} %get-tuple-element.16), channel_id=1, source_target_pairs={{0,4},{4,8},{8,12},{12,0},{1,5},{5,9},{9,13},{13,1},{2,6},{6,10},{... | collective-permute-start | bytes 638984 | tf_op jit(solution)/shard_map/ppermute | solution.py:309
  73.8 5.5 %collective-permute-start.1 = (f32[4,104,128]{2,1,0:T(8,128)}, f32[4,104,128]{2,1,0:T(8,128)}, u32[]{:S(2)}, u32[]{:S(2)}) collective-permute-start(f32[4,104,128]{2,1,0:T(8,128)} %get-tuple-element.17), channel_id=1, source_target_pairs={{0,8},{4,12},{8,0},{12,4},{1,9},{5,13},{9,1},{13,5},{2,10},{6,14},... | collective-permute-start | bytes 638984 | tf_op jit(solution)/shard_map/ppermute | solution.py:309
  79.3 1.9 collective-permute-start.2
  81.2 33.9 %collective-permute-done.refs_0_ = f32[4,104,128]{2,1,0:T(8,128)} collective-permute-done((f32[4,104,128]{2,1,0:T(8,128)}, f32[4,104,128]{2,1,0:T(8,128)}, u32[]{:S(2)}, u32[]{:S(2)}) %collective-permute-start) | collective-permute-done | bytes 213024 | tf_op jit(solution)/shard_map/ppermute | solution.py:309
  115.1 4.2 %collective-permute-done.1.refs_1_ = f32[4,104,128]{2,1,0:T(8,128)} collective-permute-done((f32[4,104,128]{2,1,0:T(8,128)}, f32[4,104,128]{2,1,0:T(8,128)}, u32[]{:S(2)}, u32[]{:S(2)}) %collective-permute-start.1) | collective-permute-done | bytes 213024 | tf_op jit(solution)/shard_map/ppermute | solution.py:309
  119.3 0.0 collective-permute-done.2.refs_2_
  119.3 1.8 add.61
  121.1 9.5 %collective-permute-start.3 = (f32[104,128]{1,0:T(8,128)}, f32[104,128]{1,0:T(8,128)S(1)}, u32[]{:S(2)}, u32[]{:S(2)}) collective-permute-start(f32[104,128]{1,0:T(8,128)} %get-tuple-element.20), channel_id=1, source_target_pairs={{0,128},{128,256},{256,384},{384,0},{1,129},{129,257},{257,385},{3... | collective-permute-start | bytes 159752 | tf_op jit(solution)/shard_map/ppermute | solution.py:309
  130.6 8.2 %collective-permute-start.4 = (f32[104,128]{1,0:T(8,128)}, f32[104,128]{1,0:T(8,128)S(1)}, u32[]{:S(2)}, u32[]{:S(2)}) collective-permute-start(f32[104,128]{1,0:T(8,128)} %get-tuple-element.21), channel_id=1, source_target_pairs={{0,256},{128,384},{256,0},{384,128},{1,257},{129,385},{257,1},{385... | collective-permute-start | bytes 159752 | tf_op jit(solution)/shard_map/ppermute | solution.py:309
  138.8 3.7 %collective-permute-start.5 = (f32[104,128]{1,0:T(8,128)}, f32[104,128]{1,0:T(8,128)S(1)}, u32[]{:S(2)}, u32[]{:S(2)}) collective-permute-start(f32[104,128]{1,0:T(8,128)} %get-tuple-element.22), channel_id=1, source_target_pairs={{0,384},{128,0},{256,128},{384,256},{1,385},{129,1},{257,129},{385... | collective-permute-start | bytes 159752 | tf_op jit(solution)/shard_map/ppermute | solution.py:309
  142.5 0.0 collective-permute-done.3.one_ref
  142.5 0.0 collective-permute-done.4.two_ref
  142.5 3.5 %collective-permute-done.5.three_ref = f32[104,128]{1,0:T(8,128)S(1)} collective-permute-done((f32[104,128]{1,0:T(8,128)}, f32[104,128]{1,0:T(8,128)S(1)}, u32[]{:S(2)}, u32[]{:S(2)}) %collective-permute-start.5) | collective-permute-done | bytes 53280 | tf_op jit(solution)/shard_map/ppermute | solution.py:309
  146.1 0.1 finish_a.1
  146.2 0.0 copy-start.5
  146.2 0.6 copy-done.5
  146.8 0.0 all-to-all-done.1.arrived_ref
  146.8 0.0 copy-start.4
  146.8 0.8 copy-done.4
  147.5 0.0 copy-start.6
  147.5 1.8 merge_b.1
  149.3 0.0 copy-start.2
  149.4 0.9 copy-done.2
  150.3 7.2 %all-to-all-start.2 = ((f32[16,104,128]{2,1,0:T(8,128)}), f32[16,104,128]{2,1,0:T(8,128)S(1)}, u32[]{:S(2)}, u32[]{:S(2)}) async-start(f32[16,104,128]{2,1,0:T(8,128)} %copy-done.2), calls=%async_computation.2 | async-start | bytes 1703936 | tf_op jit(solution)/shard_map/all_to_all | solution.py:376
  157.5 0.0 copy-done.6
  157.5 2.7 %collective-permute-start.6 = (f32[96,128]{1,0:T(8,128)S(1)}, f32[96,128]{1,0:T(8,128)S(1)}, u32[]{:S(2)}, u32[]{:S(2)}) collective-permute-start(f32[96,128]{1,0:T(8,128)S(1)} %copy-done.6), channel_id=1, source_target_pairs={{0,0},{4,64},{8,8},{12,72},{64,4},{68,68},{72,12},{76,76},{1,1},{5... | collective-permute-start | bytes 147464 | tf_op jit(solution)/shard_map/ppermute | solution.py:320
  160.2 16.6 %collective-permute-done.6 = f32[96,128]{1,0:T(8,128)S(1)} collective-permute-done((f32[96,128]{1,0:T(8,128)S(1)}, f32[96,128]{1,0:T(8,128)S(1)}, u32[]{:S(2)}, u32[]{:S(2)}) %collective-permute-start.6) | collective-permute-done | bytes 49184 | tf_op jit(solution)/shard_map/ppermute | solution.py:320
  176.8 32.0 %all-gather = f32[768,128]{1,0:T(8,128)S(1)} all-gather(f32[96,128]{1,0:T(8,128)S(1)} %collective-permute-done.6), channel_id=2, replica_groups=mesh['zp'=4,'zb'=2,'x'=4,'yp'=4,'yb'=2,'c'=2] {'zp','zb'}, dimensions={0}, use_global_device_ids=true | all-gather | bytes 442368 | tf_op jit(solution)/shard_map/all_gather | solution.py:321
  208.8 0.0 all-to-all-done.2.refs_1_
  208.8 0.2 finish_b.1
  209.0 3.1 %collective-permute-start.7 = (f32[104,128]{1,0:T(8,128)S(1)}, f32[104,128]{1,0:T(8,128)S(1)}, u32[]{:S(2)}, u32[]{:S(2)}) collective-permute-start(f32[104,128]{1,0:T(8,128)S(1)} %finish_b.1), channel_id=1, source_target_pairs={{0,0},{4,64},{8,8},{12,72},{64,4},{68,68},{72,12},{76,76},{1,1},{5... | collective-permute-start | bytes 159752 | tf_op jit(solution)/shard_map/ppermute | solution.py:320
  212.1 4.8 %collective-permute-done.7 = f32[104,128]{1,0:T(8,128)S(1)} collective-permute-done((f32[104,128]{1,0:T(8,128)S(1)}, f32[104,128]{1,0:T(8,128)S(1)}, u32[]{:S(2)}, u32[]{:S(2)}) %collective-permute-start.7) | collective-permute-done | bytes 53280 | tf_op jit(solution)/shard_map/ppermute | solution.py:320
  217.0 25.1 %all-gather.1 = f32[832,128]{1,0:T(8,128)S(1)} all-gather(f32[104,128]{1,0:T(8,128)S(1)} %collective-permute-done.7), channel_id=3, replica_groups=mesh['zp'=4,'zb'=2,'x'=4,'yp'=4,'yb'=2,'c'=2] {'zp','zb'}, dimensions={0}, use_global_device_ids=true | all-gather | bytes 479232 | tf_op jit(solution)/shard_map/all_gather | solution.py:321
  242.0 0.9 lay.1
  243.0 0.6 reshape_squeeze.3
  (9 shorter events, 0.1 us)
Async XLA Ops:
  3.3 1.9 copy-start
  9.8 8.1 %copy-start.1 = (f32[1024,768]{1,0:T(8,128)S(1)}, f32[1024,768]{1,0:T(8,128)}, u32[]{:S(2)}) copy-start(f32[1024,768]{1,0:T(8,128)} %refs_2_.3) | copy-start | bytes 9437188
  9.8 47.1 %all-to-all-start = ((f32[32,200,128]{2,1,0:T(8,128)}), f32[32,200,128]{2,1,0:T(8,128)}, u32[]{:S(2)}, u32[]{:S(2)}) async-start(f32[32,200,128]{2,1,0:T(8,128)} %pack.2), calls=%async_computation | async-start | bytes 6553600 | tf_op jit(solution)/shard_map/all_to_all | solution.py:325
  56.9 89.9 %all-to-all-start.1 = ((f32[32,200,128]{2,1,0:T(8,128)}), f32[32,200,128]{2,1,0:T(8,128)S(1)}, u32[]{:S(2)}, u32[]{:S(2)}) async-start(f32[32,200,128]{2,1,0:T(8,128)} %pack.3), calls=%async_computation.1 | async-start | bytes 6553600 | tf_op jit(solution)/shard_map/all_to_all | solution.py:325
  68.4 0.6 copy-start.3
  69.0 46.1 %collective-permute-start = (f32[4,104,128]{2,1,0:T(8,128)}, f32[4,104,128]{2,1,0:T(8,128)}, u32[]{:S(2)}, u32[]{:S(2)}) collective-permute-start(f32[4,104,128]{2,1,0:T(8,128)} %get-tuple-element.16), channel_id=1, source_target_pairs={{0,4},{4,8},{8,12},{12,0},{1,5},{5,9},{9,13},{13,1},{2,6},{6,10},{... | collective-permute-start | bytes 638984 | tf_op jit(solution)/shard_map/ppermute | solution.py:309
  73.8 45.5 %collective-permute-start.1 = (f32[4,104,128]{2,1,0:T(8,128)}, f32[4,104,128]{2,1,0:T(8,128)}, u32[]{:S(2)}, u32[]{:S(2)}) collective-permute-start(f32[4,104,128]{2,1,0:T(8,128)} %get-tuple-element.17), channel_id=1, source_target_pairs={{0,8},{4,12},{8,0},{12,4},{1,9},{5,13},{9,1},{13,5},{2,10},{6,14},... | collective-permute-start | bytes 638984 | tf_op jit(solution)/shard_map/ppermute | solution.py:309
  79.3 40.0 %collective-permute-start.2 = (f32[4,104,128]{2,1,0:T(8,128)}, f32[4,104,128]{2,1,0:T(8,128)}, u32[]{:S(2)}, u32[]{:S(2)}) collective-permute-start(f32[4,104,128]{2,1,0:T(8,128)} %get-tuple-element.18), channel_id=1, source_target_pairs={{0,12},{4,0},{8,4},{12,8},{1,13},{5,1},{9,5},{13,9},{2,14},{6,2},{... | collective-permute-start | bytes 638984 | tf_op jit(solution)/shard_map/ppermute | solution.py:309
  121.1 21.4 %collective-permute-start.3 = (f32[104,128]{1,0:T(8,128)}, f32[104,128]{1,0:T(8,128)S(1)}, u32[]{:S(2)}, u32[]{:S(2)}) collective-permute-start(f32[104,128]{1,0:T(8,128)} %get-tuple-element.20), channel_id=1, source_target_pairs={{0,128},{128,256},{256,384},{384,0},{1,129},{129,257},{257,385},{3... | collective-permute-start | bytes 159752 | tf_op jit(solution)/shard_map/ppermute | solution.py:309
  130.6 11.9 %collective-permute-start.4 = (f32[104,128]{1,0:T(8,128)}, f32[104,128]{1,0:T(8,128)S(1)}, u32[]{:S(2)}, u32[]{:S(2)}) collective-permute-start(f32[104,128]{1,0:T(8,128)} %get-tuple-element.21), channel_id=1, source_target_pairs={{0,256},{128,384},{256,0},{384,128},{1,257},{129,385},{257,1},{385... | collective-permute-start | bytes 159752 | tf_op jit(solution)/shard_map/ppermute | solution.py:309
  138.8 7.2 %collective-permute-start.5 = (f32[104,128]{1,0:T(8,128)}, f32[104,128]{1,0:T(8,128)S(1)}, u32[]{:S(2)}, u32[]{:S(2)}) collective-permute-start(f32[104,128]{1,0:T(8,128)} %get-tuple-element.22), channel_id=1, source_target_pairs={{0,384},{128,0},{256,128},{384,256},{1,385},{129,1},{257,129},{385... | collective-permute-start | bytes 159752 | tf_op jit(solution)/shard_map/ppermute | solution.py:309
  146.2 0.6 copy-start.5
  146.8 0.8 copy-start.4
  147.5 9.9 %copy-start.6 = (f32[96,128]{1,0:T(8,128)S(1)}, f32[96,128]{1,0:T(8,128)}, u32[]{:S(2)}) copy-start(f32[96,128]{1,0:T(8,128)} %copy-done.5) | copy-start | bytes 147460
  149.3 0.9 copy-start.2
  150.3 58.6 %all-to-all-start.2 = ((f32[16,104,128]{2,1,0:T(8,128)}), f32[16,104,128]{2,1,0:T(8,128)S(1)}, u32[]{:S(2)}, u32[]{:S(2)}) async-start(f32[16,104,128]{2,1,0:T(8,128)} %copy-done.2), calls=%async_computation.2 | async-start | bytes 1703936 | tf_op jit(solution)/shard_map/all_to_all | solution.py:376
  157.5 19.3 %collective-permute-start.6 = (f32[96,128]{1,0:T(8,128)S(1)}, f32[96,128]{1,0:T(8,128)S(1)}, u32[]{:S(2)}, u32[]{:S(2)}) collective-permute-start(f32[96,128]{1,0:T(8,128)S(1)} %copy-done.6), channel_id=1, source_target_pairs={{0,0},{4,64},{8,8},{12,72},{64,4},{68,68},{72,12},{76,76},{1,1},{5... | collective-permute-start | bytes 147464 | tf_op jit(solution)/shard_map/ppermute | solution.py:320
  209.0 7.9 %collective-permute-start.7 = (f32[104,128]{1,0:T(8,128)S(1)}, f32[104,128]{1,0:T(8,128)S(1)}, u32[]{:S(2)}, u32[]{:S(2)}) collective-permute-start(f32[104,128]{1,0:T(8,128)S(1)} %finish_b.1), channel_id=1, source_target_pairs={{0,0},{4,64},{8,8},{12,72},{64,4},{68,68},{72,12},{76,76},{1,1},{5... | collective-permute-start | bytes 159752 | tf_op jit(solution)/shard_map/ppermute | solution.py:320

commit v3 on v0

v3 whole, which is shorter than its diff:
```python
import jax
import jax.numpy as jnp
from jax import lax
from jax.experimental import pallas as pl
from jax.experimental.pallas import tpu as pltpu
from jax.sharding import Mesh
from jax.sharding import PartitionSpec as P

CL_OWN = 256
OWNERS = 64
LANES = 128
CAP = 32
SIDE = 4
GROUPS = OWNERS // SIDE
HALVES = 2
MERGE = GROUPS * HALVES
SLOTS = SIDE * CAP
ROWS = CL_OWN // SIDE
KEYS = MERGE * CAP
TAIL = 8


def split3(value):
    first = value.astype(jnp.bfloat16)
    rest = value - first.astype(jnp.float32)
    second = rest.astype(jnp.bfloat16)
    third = (rest - second.astype(jnp.float32)).astype(jnp.bfloat16)
    return first, second, third


def whole(space=pltpu.VMEM):
    return pl.BlockSpec(memory_space=space)


def params(mib):
    return pltpu.CompilerParams(vmem_limit_bytes=mib * 1024 * 1024)


def pack_kernel(row_ref, points_ref, tags_ref, out_ref):
    rows, width = points_ref.shape
    blocks = width // LANES // HALVES
    stride = blocks * SLOTS + TAIL
    flat = out_ref.reshape(MERGE * stride, LANES)

    def clear(g, carry):
        start = pl.multiple_of(g * stride, 8)
        flat[pl.ds(start, stride - TAIL), :] = jnp.zeros((stride - TAIL, LANES), jnp.float32)
        flat[pl.ds(start + stride - TAIL, TAIL), :] = tags_ref[g & (GROUPS - 1)]
        return carry

    lax.fori_loop(0, MERGE, clear, 0)

    def place(i, carry):
        start = pl.multiple_of(i * 8, 8)
        ats = [row_ref[i * 8 + r] for r in range(8)]
        for h in range(HALVES):
            for j in range(blocks):
                low = (h * blocks + j) * LANES
                tile = points_ref[pl.ds(start, 8), low : low + LANES]
                for r in range(8):
                    at = ats[r] + (h * GROUPS * stride + j * SLOTS)
                    flat[pl.ds(at, 1), :] = tile[r : r + 1]
        return carry

    lax.fori_loop(0, rows // 8, place, 0)


def pack(row, points, tags):
    blocks = points.shape[1] // LANES // HALVES
    return pl.pallas_call(
        pack_kernel,
        out_shape=jax.ShapeDtypeStruct((MERGE, blocks * SLOTS + TAIL, LANES), jnp.float32),
        in_specs=[whole(pltpu.SMEM), whole(), whole()],
        out_specs=whole(),
        compiler_params=params(12),
        name="pack",
    )(row, points, tags)


def merge_kernel(arrived_ref, out_ref, hot_ref, square_ref):
    blocks = (arrived_ref.shape[1] - TAIL) // SLOTS
    tail = blocks * SLOTS
    gather = LANES // CAP
    tiles = []
    for k in range(MERGE // gather):
        tile = arrived_ref[k * gather, tail:, :]
        for s in range(1, gather):
            tile = tile + arrived_ref[k * gather + s, tail:, :]
        tiles.append(tile)
    tags = jnp.concatenate(tiles, axis=1).astype(jnp.int32)
    cluster = lax.broadcasted_iota(jnp.int32, (CL_OWN, KEYS), 0) + 1
    for m in range(SIDE):
        hot = (cluster == tags[m : m + 1]).astype(jnp.float32).astype(jnp.bfloat16)
        hot_ref[m] = hot
        for j in range(blocks):
            low = j * SLOTS + m * CAP
            data = arrived_ref[:, low : low + CAP, :].reshape(KEYS, LANES)
            squares = data * data
            square_ref[...] = squares if j == 0 else square_ref[...] + squares
            terms = jnp.concatenate(split3(data), axis=1)
            total = jnp.dot(hot_ref[m], terms, preferred_element_type=jnp.float32)
            total = total[:, 2 * LANES :] + total[:, LANES : 2 * LANES] + total[:, :LANES]
            for zp in range(SIDE):
                out_ref[m * SIDE + zp, j * ROWS : (j + 1) * ROWS, :] = total[
                    zp * ROWS : (zp + 1) * ROWS
                ]
        ones = jnp.ones((TAIL, LANES), jnp.bfloat16)
        norms = sum(
            lax.dot_general(
                ones, term, (((1,), (1,)), ((), ())), preferred_element_type=jnp.float32
            )
            for term in reversed(split3(square_ref[...]))
        )
        row = lax.broadcasted_iota(jnp.int32, (TAIL, KEYS), 0)
        values = jnp.where(row == 0, 1.0, 0.0)
        for k, term in enumerate(split3(norms), 1):
            values = jnp.where(row == k, term.astype(jnp.float32), values)
        small = lax.dot_general(
            values.astype(jnp.bfloat16),
            hot_ref[m],
            (((1,), (1,)), ((), ())),
            preferred_element_type=jnp.float32,
        )
        for zp in range(SIDE):
            low = zp * ROWS // LANES * LANES
            out_ref[m * SIDE + zp, blocks * ROWS :, :] = small[:, low : low + LANES]


def merge(arrived):
    blocks = (arrived.shape[1] - TAIL) // SLOTS
    return pl.pallas_call(
        merge_kernel,
        out_shape=jax.ShapeDtypeStruct((SIDE * SIDE, blocks * ROWS + TAIL, LANES), jnp.float32),
        in_specs=[whole()],
        out_specs=whole(),
        scratch_shapes=[
            pltpu.VMEM((SIDE, CL_OWN, KEYS), jnp.bfloat16),
            pltpu.VMEM((KEYS, LANES), jnp.float32),
        ],
        compiler_params=params(16),
        name="merge",
    )(arrived)


def finish_kernel(offset_ref, arrived_ref, out_ref):
    total = arrived_ref[0]
    for k in range(1, SIDE * SIDE):
        total = total + arrived_ref[k]
    tail = total.shape[0] - TAIL
    row = lax.broadcasted_iota(jnp.int32, (ROWS, LANES), 0)
    lane = lax.broadcasted_iota(jnp.int32, (ROWS, LANES), 1)
    mine = lane == row + offset_ref[0]
    counts = jnp.sum(jnp.where(mine, total[tail : tail + 1], 0.0), axis=1, keepdims=True)
    denom = jnp.maximum(counts, 1.0)
    norm = jnp.zeros((ROWS, LANES), jnp.float32)
    for low in range(0, tail, ROWS):
        sums = total[low : low + ROWS]
        norm = norm + sums * sums
        out_ref[low : low + ROWS, :] = sums / denom
    norm = jnp.sum(norm, axis=1, keepdims=True)
    norm = jnp.sum(jnp.where(mine, norm, 0.0), axis=0, keepdims=True)
    squares = total[tail + 1 : tail + 2] + total[tail + 2 : tail + 3] + total[tail + 3 : tail + 4]
    line = lax.broadcasted_iota(jnp.int32, (TAIL, LANES), 0)
    last = jnp.where(line == 0, total[tail : tail + 1], 0.0)
    last = jnp.where(line == 1, squares, last)
    out_ref[tail:, :] = jnp.where(line == 2, norm, last)


def finish(offset, arrived):
    return pl.pallas_call(
        finish_kernel,
        out_shape=jax.ShapeDtypeStruct(arrived.shape[1:], jnp.float32),
        in_specs=[whole(pltpu.SMEM), whole()],
        out_specs=whole(),
        compiler_params=params(6),
        name="finish",
    )(offset, arrived)


def lay_kernel(all_ref, centre_ref, spread_ref):
    width = centre_ref.shape[1]
    blocks = width // LANES // HALVES
    tail = blocks * ROWS
    for zp in range(SIDE):
        for zb in range(HALVES):
            for j in range(blocks):
                low = (zb * blocks + j) * LANES
                centre_ref[zp * ROWS : (zp + 1) * ROWS, low : low + LANES] = all_ref[
                    zp * HALVES + zb, j * ROWS : (j + 1) * ROWS, :
                ]
    share = LANES // ROWS
    for t in range(SIDE // share):
        first = t * share * HALVES
        denom = jnp.maximum(all_ref[first, tail : tail + 1, :], 1.0)
        squares = sum(all_ref[first + zb, tail + 1 : tail + 2, :] for zb in range(HALVES))
        norm = sum(all_ref[first + k, tail + 2 : tail + 3, :] for k in range(share * HALVES))
        spread_ref[t : t + 1, :] = (squares - norm / denom) / (denom * width)


def lay(gathered, width):
    return pl.pallas_call(
        lay_kernel,
        out_shape=[
            jax.ShapeDtypeStruct((CL_OWN, width), jnp.float32),
            jax.ShapeDtypeStruct((CL_OWN // LANES, LANES), jnp.float32),
        ],
        in_specs=[whole()],
        out_specs=[whole(), whole()],
        compiler_params=params(6),
        name="lay",
    )(gathered)


def body(points, assignment):
    rows, width = points.shape
    owner = assignment >> 8
    label = assignment & (CL_OWN - 1)
    slot = ((owner >> 4) * 4 + (owner & 3)) * SIDE + ((owner >> 2) & 3)
    matches = slot[:, None] == jnp.arange(OWNERS, dtype=jnp.int32)[None, :]
    matches = matches.astype(jnp.float32)
    earlier = (jnp.arange(rows)[:, None] > jnp.arange(rows)[None, :]).astype(jnp.float32)
    before = jnp.dot(earlier, matches, preferred_element_type=jnp.float32)
    position = jnp.sum(before * matches, axis=1).astype(jnp.int32)
    stride = width // LANES // HALVES * SLOTS + TAIL
    row = (slot // SIDE) * stride + (slot % SIDE) * CAP + position
    at = position[:, None] == jnp.arange(CAP, dtype=jnp.int32)[None, :]
    placed = lax.dot_general(
        matches,
        jnp.where(at, (label + 1).astype(jnp.float32)[:, None], 0.0),
        (((0,), (0,)), ((), ())),
        preferred_element_type=jnp.float32,
    )
    share = LANES // CAP
    group = (lax.axis_index("yb") * 2 + lax.axis_index("c")) % share
    lanes = jnp.arange(LANES, dtype=jnp.int32)[None, None, :] // CAP == group
    tags = jnp.where(lanes, jnp.tile(placed.reshape(GROUPS, SIDE, CAP), (1, 1, share)), 0.0)
    tags = jnp.pad(tags, ((0, 0), (0, TAIL - SIDE), (0, 0)))

    packed = pack(row, points, tags)
    met = lax.all_to_all(packed, ("zb", "x", "yb", "c"), split_axis=0, concat_axis=0, tiled=True)
    partial = merge(met)
    partial = lax.all_to_all(partial, ("yp", "zp"), split_axis=0, concat_axis=0, tiled=True)
    offset = (lax.axis_index("zp") * ROWS % LANES).reshape(1)
    done = finish(offset, partial)
    gathered = lax.all_gather(done, ("zp", "zb"), axis=0, tiled=False)
    centre, spread = lay(gathered, width)
    return centre, spread.reshape(CL_OWN)


def solution(mesh):
    fine = Mesh(mesh.devices.reshape(4, 2, 4, 4, 2, 2), ("zp", "zb", "x", "yp", "yb", "c"))
    every = ("zp", "zb", "x", "yp", "yb", "c")
    owners = ("x", "yp", "yb", "c")
    return jax.shard_map(
        body,
        mesh=fine,
        in_specs=(P(every, None), P(every)),
        out_specs=(P(owners, None), P(owners)),
        check_vma=False,
    )
```

time: 254 us -> 189 us (0.74)
  waiting for transfers between devices: 138 us -> 49.9 us
  blocking collectives: 64 us -> 108 us
  local copies, waits for them, and re-layouts: 16.2 us -> 2.05 us
  Pallas kernels: 0 us -> 12.6 us
  starting transfers between devices: 21.2 us -> 12.8 us
  matrix products: 7.85 us -> 1.06 us
  other arithmetic: 6.18 us -> 1.43 us
    all_to_all x2 -> x1, waiting for transfers between devices: 138 us -> 49.9 us  [body(): lax.all_to_all(partial, ('yp', 'zp'), split_axis=0, concat_axis=0, tiled=...]
    all_to_all x1, blocking collectives: 37.4 us -> 82.4 us  [body(): lax.all_to_all(packed, ('zb', 'x', 'yb', 'c'), split_axis=0, concat_axis=...]
    scatter x2 -> x0, local copies, waits for them, and re-layouts: 13 us -> none  [the longest x1 8.66 us: body(): jnp.zeros((owners * capacity, width), jnp.float32).at[target].set(points)]
    pallas_call x0 -> x4, Pallas kernels: none -> 12.6 us  [the longest x1 6.4 us: merge(): pl.pallas_call(merge_kernel, out_shape=jax.ShapeDtypeStruct((SIDE * SIDE,...]
    all_to_all x2 -> x1, starting transfers between devices: 21.2 us -> 12.8 us  [body(): lax.all_to_all(partial, ('yp', 'zp'), split_axis=0, concat_axis=0, tiled=...]
    dot_general x2 -> x1, matrix products: 7.25 us -> 0.47 us  [body(): lax.dot_general(matches, jnp.where(at, (label + 1).astype(jnp.float32)[:,...]
    reduce_sum x3 -> x0, other arithmetic: 3.59 us -> none  [the longest x1 3.25 us: body(): jnp.sum(arrived * arrived, axis=1)]
  transfers between devices with their start and end apart: 2 -> 1, of which waited for: 1 -> 1; matrix products, arithmetic and copies ran while one was open for 4% -> 0% of each run, Pallas kernels for 0% -> 0%
where the time goes in v3:
time: 189 us
  blocking collectives  108 us (57%)
  waiting for transfers between devices  49.9 us (26%)
  starting transfers between devices  12.8 us (7%)
  Pallas kernels  12.6 us (7%)
  local copies, waits for them, and re-layouts  2.05 us (1%)
    all_to_all x1, blocking collectives, body(): lax.all_to_all(packed, ('zb', 'x', 'yb', 'c'), split_axis=0, concat_axis=...  82.4 us
    all_to_all x1, waiting for transfers between devices, body(): lax.all_to_all(partial, ('yp', 'zp'), split_axis=0, concat_axis=0, tiled=...  49.9 us
    all_gather x1, blocking collectives, body(): gathered = lax.all_gather(done, ('zp', 'zb'), axis=0, tiled=False)  26.1 us
    all_to_all x1, starting transfers between devices, body(): lax.all_to_all(partial, ('yp', 'zp'), split_axis=0, concat_axis=0, tiled=...  12.8 us
    pallas_call x1, Pallas kernels, merge(): pl.pallas_call(merge_kernel, out_shape=jax.ShapeDtypeStruct((SIDE * SIDE,...  6.4 us
    pallas_call x1, Pallas kernels, pack(): pl.pallas_call(pack_kernel, out_shape=jax.ShapeDtypeStruct((MERGE, blocks...  5.06 us
  transfers between devices with their start and end apart: 1, of which 1 were waited for; matrix products, arithmetic and copies ran while one was open for 0% of the time, Pallas kernels for 0%

profile of v3, /device:TPU:2, one launch (start us, length us, event | category | flops | bytes accessed | tf_op | source)
XLA Modules:
  0.0 189.0 jit_solution(3192962297143920578)
XLA Ops:
  0.6 0.7 and_add_fusion
  1.3 0.6 fusion.2
  2.0 0.7 add_convert_fusion
  2.7 0.5 fusion.3
  3.2 0.1 tile.12
  3.4 0.0 copy-start
  3.4 1.9 copy-done
  5.2 5.1 %pack.1 = f32[32,392,128]{2,1,0:T(8,128)S(1)} custom-call(s32[1024]{0:T(1024)S(1)} %get-tuple-element.7.row_ref, f32[1024,768]{1,0:T(8,128)S(1)} %copy-done, f32[16,8,128]{2,1,0:T(8,128)S(1)} %pad.4.tags_ref), custom_call_target="tpu_custom_call" | custom-call | tf_op jit(solution)/shard_map/pack/pallas_call | solution.py:70
  10.3 82.4 %all_to_all.10.arrived_ref = f32[32,392,128]{2,1,0:T(8,128)S(1)} all-to-all(f32[32,392,128]{2,1,0:T(8,128)S(1)} %pack.1), channel_id=1, replica_groups=mesh['zp'=4,'zb'=2,'x'=4,'yp'=4,'yb'=2,'c'=2] {'zb','x','yb','c'}, dimensions={0} | all-to-all | bytes 12845056 | tf_op jit(solution)/shard_map/all_to_all | solution.py:240
  92.7 6.4 %merge.1 = f32[16,200,128]{2,1,0:T(8,128)} custom-call(f32[32,392,128]{2,1,0:T(8,128)S(1)} %all_to_all.10.arrived_ref), custom_call_target="tpu_custom_call" | custom-call | tf_op jit(solution)/shard_map/merge/pallas_call | solution.py:131
  99.1 12.8 %all-to-all-start.1 = ((f32[16,200,128]{2,1,0:T(8,128)}), f32[16,200,128]{2,1,0:T(8,128)S(1)}, u32[]{:S(2)}, u32[]{:S(2)}) async-start(f32[16,200,128]{2,1,0:T(8,128)} %merge.1), calls=%async_computation.1 | async-start | bytes 3276800 | tf_op jit(solution)/shard_map/all_to_all | solution.py:242
  111.9 49.9 %all-to-all-done.1.arrived_ref = f32[16,200,128]{2,1,0:T(8,128)S(1)} async-done(((f32[16,200,128]{2,1,0:T(8,128)}), f32[16,200,128]{2,1,0:T(8,128)S(1)}, u32[]{:S(2)}, u32[]{:S(2)}) %all-to-all-start.1) | async-done | bytes 1638432 | tf_op jit(solution)/shard_map/all_to_all | solution.py:242
  161.9 0.2 finish.1
  162.0 26.1 %all-gather = f32[1600,128]{1,0:T(8,128)S(1)} all-gather(f32[200,128]{1,0:T(8,128)S(1)} %finish.1), channel_id=2, replica_groups=mesh['zp'=4,'zb'=2,'x'=4,'yp'=4,'yb'=2,'c'=2] {'zp','zb'}, dimensions={0}, use_global_device_ids=true | all-gather | bytes 921600 | tf_op jit(solution)/shard_map/all_gather | solution.py:245
  188.1 0.9 lay.1
  (5 shorter events, 0.1 us)
Async XLA Ops:
  3.4 1.9 %copy-start = (f32[1024,768]{1,0:T(8,128)S(1)}, f32[1024,768]{1,0:T(8,128)}, u32[]{:S(2)}) copy-start(f32[1024,768]{1,0:T(8,128)} %points_ref.1) | copy-start | bytes 9437188
  99.1 62.8 %all-to-all-start.1 = ((f32[16,200,128]{2,1,0:T(8,128)}), f32[16,200,128]{2,1,0:T(8,128)S(1)}, u32[]{:S(2)}, u32[]{:S(2)}) async-start(f32[16,200,128]{2,1,0:T(8,128)} %merge.1), calls=%async_computation.1 | async-start | bytes 3276800 | tf_op jit(solution)/shard_map/all_to_all | solution.py:242

commit v4 on v3

--- a/solution.py
+++ b/solution.py
@@ -18,6 +18,7 @@
 ROWS = CL_OWN // SIDE
 KEYS = MERGE * CAP
 TAIL = 8
+PIECES = 4
 
 
 def split3(value):
@@ -36,8 +37,17 @@
     return pltpu.CompilerParams(vmem_limit_bytes=mib * 1024 * 1024)
 
 
-def pack_kernel(row_ref, points_ref, tags_ref, out_ref):
+def pack_kernel(row_ref, given_ref, tags_ref, out_ref, points_ref, sems):
     rows, width = points_ref.shape
+    piece = rows // PIECES
+    copies = [
+        pltpu.make_async_copy(
+            given_ref.at[pl.ds(k * piece, piece)], points_ref.at[pl.ds(k * piece, piece)], sems.at[k]
+        )
+        for k in range(PIECES)
+    ]
+    for copy in copies:
+        copy.start()
     blocks = width // LANES // HALVES
     stride = blocks * SLOTS + TAIL
     flat = out_ref.reshape(MERGE * stride, LANES)
@@ -62,7 +72,9 @@
                     flat[pl.ds(at, 1), :] = tile[r : r + 1]
         return carry
 
-    lax.fori_loop(0, rows // 8, place, 0)
+    for k, copy in enumerate(copies):
+        copy.wait()
+        lax.fori_loop(k * piece // 8, (k + 1) * piece // 8, place, 0)
 
 
 def pack(row, points, tags):
@@ -70,8 +82,12 @@
     return pl.pallas_call(
         pack_kernel,
         out_shape=jax.ShapeDtypeStruct((MERGE, blocks * SLOTS + TAIL, LANES), jnp.float32),
-        in_specs=[whole(pltpu.SMEM), whole(), whole()],
-        out_specs=whole(),
+        in_specs=[whole(pltpu.SMEM), whole(pltpu.HBM), whole()],
+        out_specs=whole(),
+        scratch_shapes=[
+            pltpu.VMEM(points.shape, jnp.float32),
+            pltpu.SemaphoreType.DMA((PIECES,)),
+        ],
         compiler_params=params(12),
         name="pack",
     )(row, points, tags)
@@ -142,10 +158,23 @@
     )(arrived)
 
 
+def add_kernel(arrived_ref, out_ref):
+    out_ref[...] = (arrived_ref[0] + arrived_ref[1]) + (arrived_ref[2] + arrived_ref[3])
+
+
+def add(arrived):
+    return pl.pallas_call(
+        add_kernel,
+        out_shape=jax.ShapeDtypeStruct(arrived.shape[1:], jnp.float32),
+        in_specs=[whole()],
+        out_specs=whole(),
+        compiler_params=params(6),
+        name="add",
+    )(arrived)
+
+
 def finish_kernel(offset_ref, arrived_ref, out_ref):
-    total = arrived_ref[0]
-    for k in range(1, SIDE * SIDE):
-        total = total + arrived_ref[k]
+    total = (arrived_ref[0] + arrived_ref[1]) + (arrived_ref[2] + arrived_ref[3])
     tail = total.shape[0] - TAIL
     row = lax.broadcasted_iota(jnp.int32, (ROWS, LANES), 0)
     lane = lax.broadcasted_iota(jnp.int32, (ROWS, LANES), 1)
@@ -156,20 +185,24 @@
     for low in range(0, tail, ROWS):
         sums = total[low : low + ROWS]
         norm = norm + sums * sums
-        out_ref[low : low + ROWS, :] = sums / denom
+        means = sums / denom
+        for k in range(out_ref.shape[0]):
+            out_ref[k, low : low + ROWS, :] = means
     norm = jnp.sum(norm, axis=1, keepdims=True)
     norm = jnp.sum(jnp.where(mine, norm, 0.0), axis=0, keepdims=True)
     squares = total[tail + 1 : tail + 2] + total[tail + 2 : tail + 3] + total[tail + 3 : tail + 4]
     line = lax.broadcasted_iota(jnp.int32, (TAIL, LANES), 0)
     last = jnp.where(line == 0, total[tail : tail + 1], 0.0)
     last = jnp.where(line == 1, squares, last)
-    out_ref[tail:, :] = jnp.where(line == 2, norm, last)
+    last = jnp.where(line == 2, norm, last)
+    for k in range(out_ref.shape[0]):
+        out_ref[k, tail:, :] = last
 
 
 def finish(offset, arrived):
     return pl.pallas_call(
         finish_kernel,
-        out_shape=jax.ShapeDtypeStruct(arrived.shape[1:], jnp.float32),
+        out_shape=jax.ShapeDtypeStruct((SIDE * HALVES, *arrived.shape[1:]), jnp.float32),
         in_specs=[whole(pltpu.SMEM), whole()],
         out_specs=whole(),
         compiler_params=params(6),
@@ -239,10 +272,13 @@
     packed = pack(row, points, tags)
     met = lax.all_to_all(packed, ("zb", "x", "yb", "c"), split_axis=0, concat_axis=0, tiled=True)
     partial = merge(met)
-    partial = lax.all_to_all(partial, ("yp", "zp"), split_axis=0, concat_axis=0, tiled=True)
+    partial = partial.reshape(SIDE, -1, LANES)
+    partial = lax.all_to_all(partial, "yp", split_axis=0, concat_axis=0, tiled=True)
+    partial = add(partial).reshape(SIDE, -1, LANES)
+    partial = lax.all_to_all(partial, "zp", split_axis=0, concat_axis=0, tiled=True)
     offset = (lax.axis_index("zp") * ROWS % LANES).reshape(1)
     done = finish(offset, partial)
-    gathered = lax.all_gather(done, ("zp", "zb"), axis=0, tiled=False)
+    gathered = lax.all_to_all(done, ("zp", "zb"), split_axis=0, concat_axis=0, tiled=True)
     centre, spread = lay(gathered, width)
     return centre, spread.reshape(CL_OWN)
 

time: 189 us -> 195 us (1.032)
  the two profiles are of different devices: /device:TPU:2 before, /device:TPU:16 now
where the time goes in v4:
time: 195 us
  blocking collectives  155 us (79%)
  waiting for transfers between devices  13 us (7%)
  Pallas kernels  12.4 us (6%)
  starting transfers between devices  9.4 us (5%)
  local copies, waits for them, and re-layouts  2.05 us (1%)
    all_to_all x1, blocking collectives, body(): lax.all_to_all(packed, ('zb', 'x', 'yb', 'c'), split_axis=0, concat_axis=...  82.3 us
    all_to_all x1, blocking collectives, body(): lax.all_to_all(partial, 'yp', split_axis=0, concat_axis=0, tiled=True)  45.4 us
    all_to_all x1, blocking collectives, body(): lax.all_to_all(done, ('zp', 'zb'), split_axis=0, concat_axis=0, tiled=True)  27.1 us
    all_to_all x1, waiting for transfers between devices, body(): lax.all_to_all(partial, 'zp', split_axis=0, concat_axis=0, tiled=True)  13 us
    all_to_all x1, starting transfers between devices, body(): lax.all_to_all(partial, 'zp', split_axis=0, concat_axis=0, tiled=True)  9.4 us
    pallas_call x1, Pallas kernels, pack(): pl.pallas_call(pack_kernel, out_shape=jax.ShapeDtypeStruct((MERGE, blocks...  5.3 us
    pallas_call x1, Pallas kernels, merge(): pl.pallas_call(merge_kernel, out_shape=jax.ShapeDtypeStruct((SIDE * SIDE,...  5.19 us
  transfers between devices with their start and end apart: 1, of which 1 were waited for; matrix products, arithmetic and copies ran while one was open for 0% of the time, Pallas kernels for 0%

profile of v4, /device:TPU:16, one launch (start us, length us, event | category | flops | bytes accessed | tf_op | source)
XLA Modules:
  0.0 194.9 jit_solution(16755086639319876665)
XLA Ops:
  0.6 0.7 and_add_fusion
  1.3 0.6 fusion.2
  2.0 0.7 add_convert_fusion
  2.7 0.5 fusion.3
  3.2 0.1 tile.12
  3.4 0.0 copy-start
  3.4 1.9 copy-done
  5.2 5.3 %pack.1 = f32[32,392,128]{2,1,0:T(8,128)S(1)} custom-call(s32[1024]{0:T(1024)S(1)} %get-tuple-element.7.row_ref, f32[1024,768]{1,0:T(8,128)S(1)} %copy-done, f32[16,8,128]{2,1,0:T(8,128)S(1)} %pad.4.tags_ref), custom_call_target="tpu_custom_call" | custom-call | tf_op jit(solution)/shard_map/pack/pallas_call | solution.py:82
  10.6 82.3 %all_to_all.20.arrived_ref = f32[32,392,128]{2,1,0:T(8,128)S(1)} all-to-all(f32[32,392,128]{2,1,0:T(8,128)S(1)} %pack.1), channel_id=1, replica_groups=mesh['zp'=4,'zb'=2,'x'=4,'yp'=4,'yb'=2,'c'=2] {'zb','x','yb','c'}, dimensions={0} | all-to-all | bytes 12845056 | tf_op jit(solution)/shard_map/all_to_all | solution.py:273
  92.9 5.2 %merge.1 = f32[16,200,128]{2,1,0:T(8,128)S(1)} custom-call(f32[32,392,128]{2,1,0:T(8,128)S(1)} %all_to_all.20.arrived_ref), custom_call_target="tpu_custom_call" | custom-call | tf_op jit(solution)/shard_map/merge/pallas_call | solution.py:147
  98.0 45.4 %all_to_all.21.arrived_ref = f32[4,800,128]{2,1,0:T(8,128)S(1)} all-to-all(f32[4,800,128]{2,1,0:T(8,128)S(1)} %bitcast.5), channel_id=1, replica_groups=mesh['zp'=4,'zb'=2,'x'=4,'yp'=4,'yb'=2,'c'=2] {'yp'}, dimensions={0} | all-to-all | bytes 3276800 | tf_op jit(solution)/shard_map/all_to_all | solution.py:276
  143.4 0.8 add.67
  144.3 9.4 %all-to-all-start.2 = ((f32[4,200,128]{2,1,0:T(8,128)}), f32[4,200,128]{2,1,0:T(8,128)S(1)}, u32[]{:S(2)}, u32[]{:S(2)}) async-start(f32[4,200,128]{2,1,0:T(8,128)} %bitcast.3), calls=%async_computation.2 | async-start | bytes 819200 | tf_op jit(solution)/shard_map/all_to_all | solution.py:278
  153.7 13.0 %all-to-all-done.2.arrived_ref = f32[4,200,128]{2,1,0:T(8,128)S(1)} async-done(((f32[4,200,128]{2,1,0:T(8,128)}), f32[4,200,128]{2,1,0:T(8,128)S(1)}, u32[]{:S(2)}, u32[]{:S(2)}) %all-to-all-start.2) | async-done | bytes 409632 | tf_op jit(solution)/shard_map/all_to_all | solution.py:278
  166.7 0.2 finish.1
  166.9 27.1 %all_to_all.22.all_ref = f32[8,200,128]{2,1,0:T(8,128)S(1)} all-to-all(f32[8,200,128]{2,1,0:T(8,128)S(1)} %finish.1), channel_id=1, replica_groups=mesh['zp'=4,'zb'=2,'x'=4,'yp'=4,'yb'=2,'c'=2] {'zp','zb'}, dimensions={0} | all-to-all | bytes 1638400 | tf_op jit(solution)/shard_map/all_to_all | solution.py:281
  194.0 0.9 lay.1
  (5 shorter events, 0.1 us)
Async XLA Ops:
  3.4 1.9 copy-start
  144.3 22.4 %all-to-all-start.2 = ((f32[4,200,128]{2,1,0:T(8,128)}), f32[4,200,128]{2,1,0:T(8,128)S(1)}, u32[]{:S(2)}, u32[]{:S(2)}) async-start(f32[4,200,128]{2,1,0:T(8,128)} %bitcast.3), calls=%async_computation.2 | async-start | bytes 819200 | tf_op jit(solution)/shard_map/all_to_all | solution.py:278

commit v5 on v3

--- a/solution.py
+++ b/solution.py
@@ -18,6 +18,8 @@
 ROWS = CL_OWN // SIDE
 KEYS = MERGE * CAP
 TAIL = 8
+PIECES = 4
+PACK_MIB = 12
 
 
 def split3(value):
@@ -36,23 +38,69 @@
     return pltpu.CompilerParams(vmem_limit_bytes=mib * 1024 * 1024)
 
 
-def pack_kernel(row_ref, points_ref, tags_ref, out_ref):
+def pack_kernel(group_ref, assignment_ref, given_ref, flat, points_ref, rows_ref, at_ref, sems):
     rows, width = points_ref.shape
+    piece = rows // PIECES
+    copies = [
+        pltpu.make_async_copy(
+            given_ref.at[pl.ds(k * piece, piece)], points_ref.at[pl.ds(k * piece, piece)], sems.at[k]
+        )
+        for k in range(PIECES)
+    ]
+    for copy in copies:
+        copy.start()
+
     blocks = width // LANES // HALVES
     stride = blocks * SLOTS + TAIL
-    flat = out_ref.reshape(MERGE * stride, LANES)
+    earlier = lax.broadcasted_iota(jnp.int32, (LANES, LANES), 0)
+    lane = lax.broadcasted_iota(jnp.int32, (LANES, LANES), 1)
+    earlier = (earlier < lane).astype(jnp.float32).astype(jnp.bfloat16)
+    line = lax.broadcasted_iota(jnp.int32, (OWNERS, LANES), 0)
+    place = lax.broadcasted_iota(jnp.int32, (LANES, LANES), 0)
+    seen = jnp.zeros((OWNERS, 1), jnp.float32)
+    tags = jnp.zeros((OWNERS, LANES), jnp.float32)
+    for i in range(rows // LANES):
+        assigned = assignment_ref[i : i + 1, :]
+        owner = assigned >> 8
+        label = (assigned & (CL_OWN - 1)) + 1
+        group = (owner >> 4) * 4 + (owner & 3)
+        member = (owner >> 2) & 3
+        hot = (line == group * SIDE + member).astype(jnp.float32)
+        before = jnp.dot(
+            hot.astype(jnp.bfloat16), earlier, preferred_element_type=jnp.float32
+        )
+        position = jnp.sum(hot * (before + seen), axis=0, keepdims=True).astype(jnp.int32)
+        seen = seen + jnp.sum(hot, axis=1, keepdims=True)
+        rows_ref[i : i + 1, :] = group * stride + member * CAP + position
+        at = (place == position + group_ref[0] * CAP).astype(jnp.float32)
+        tags = tags + lax.dot_general(
+            (hot * label.astype(jnp.float32)).astype(jnp.bfloat16),
+            at.astype(jnp.bfloat16),
+            (((1,), (1,)), ((), ())),
+            preferred_element_type=jnp.float32,
+        )
+    listing = pltpu.make_async_copy(rows_ref, at_ref, sems.at[PIECES])
+    listing.start()
+
+    for g in range(MERGE):
+        low = (g + 1) * stride - TAIL
+        owners = (g % GROUPS) * SIDE
+        flat[low : low + SIDE, :] = tags[owners : owners + SIDE]
+        flat[low + SIDE : low + TAIL, :] = jnp.zeros((TAIL - SIDE, LANES), jnp.float32)
 
     def clear(g, carry):
         start = pl.multiple_of(g * stride, 8)
         flat[pl.ds(start, stride - TAIL), :] = jnp.zeros((stride - TAIL, LANES), jnp.float32)
-        flat[pl.ds(start + stride - TAIL, TAIL), :] = tags_ref[g & (GROUPS - 1)]
         return carry
 
     lax.fori_loop(0, MERGE, clear, 0)
-
-    def place(i, carry):
+    listing.wait()
+
+    def put(i, carry):
         start = pl.multiple_of(i * 8, 8)
-        ats = [row_ref[i * 8 + r] for r in range(8)]
+        line = i >> 4
+        first = (i & 15) * 8
+        ats = [at_ref[line, first + r] for r in range(8)]
         for h in range(HALVES):
             for j in range(blocks):
                 low = (h * blocks + j) * LANES
@@ -62,19 +110,30 @@
                     flat[pl.ds(at, 1), :] = tile[r : r + 1]
         return carry
 
-    lax.fori_loop(0, rows // 8, place, 0)
-
-
-def pack(row, points, tags):
-    blocks = points.shape[1] // LANES // HALVES
-    return pl.pallas_call(
+    for k, copy in enumerate(copies):
+        copy.wait()
+        lax.fori_loop(k * piece // 8, (k + 1) * piece // 8, put, 0)
+
+
+def pack(group, assignment, points):
+    rows, width = points.shape
+    stride = width // LANES // HALVES * SLOTS + TAIL
+    lines = (rows // LANES, LANES)
+    packed = pl.pallas_call(
         pack_kernel,
-        out_shape=jax.ShapeDtypeStruct((MERGE, blocks * SLOTS + TAIL, LANES), jnp.float32),
-        in_specs=[whole(pltpu.SMEM), whole(), whole()],
+        out_shape=jax.ShapeDtypeStruct((MERGE * stride, LANES), jnp.float32),
+        in_specs=[whole(pltpu.SMEM), whole(), whole(pltpu.HBM)],
         out_specs=whole(),
-        compiler_params=params(12),
+        scratch_shapes=[
+            pltpu.VMEM(points.shape, jnp.float32),
+            pltpu.VMEM(lines, jnp.int32),
+            pltpu.SMEM(lines, jnp.int32),
+            pltpu.SemaphoreType.DMA((PIECES + 1,)),
+        ],
+        compiler_params=params(PACK_MIB),
         name="pack",
-    )(row, points, tags)
+    )(group, assignment.reshape(lines), pltpu.with_memory_space_constraint(points, pltpu.HBM))
+    return packed.reshape(MERGE, stride, LANES)
 
 
 def merge_kernel(arrived_ref, out_ref, hot_ref, square_ref):
@@ -101,7 +160,7 @@
             total = jnp.dot(hot_ref[m], terms, preferred_element_type=jnp.float32)
             total = total[:, 2 * LANES :] + total[:, LANES : 2 * LANES] + total[:, :LANES]
             for zp in range(SIDE):
-                out_ref[m * SIDE + zp, j * ROWS : (j + 1) * ROWS, :] = total[
+                out_ref[zp * SIDE + m, j * ROWS : (j + 1) * ROWS, :] = total[
                     zp * ROWS : (zp + 1) * ROWS
                 ]
         ones = jnp.ones((TAIL, LANES), jnp.bfloat16)
@@ -123,7 +182,7 @@
         )
         for zp in range(SIDE):
             low = zp * ROWS // LANES * LANES
-            out_ref[m * SIDE + zp, blocks * ROWS :, :] = small[:, low : low + LANES]
+            out_ref[zp * SIDE + m, blocks * ROWS :, :] = small[:, low : low + LANES]
 
 
 def merge(arrived):
@@ -212,34 +271,12 @@
 
 
 def body(points, assignment):
-    rows, width = points.shape
-    owner = assignment >> 8
-    label = assignment & (CL_OWN - 1)
-    slot = ((owner >> 4) * 4 + (owner & 3)) * SIDE + ((owner >> 2) & 3)
-    matches = slot[:, None] == jnp.arange(OWNERS, dtype=jnp.int32)[None, :]
-    matches = matches.astype(jnp.float32)
-    earlier = (jnp.arange(rows)[:, None] > jnp.arange(rows)[None, :]).astype(jnp.float32)
-    before = jnp.dot(earlier, matches, preferred_element_type=jnp.float32)
-    position = jnp.sum(before * matches, axis=1).astype(jnp.int32)
-    stride = width // LANES // HALVES * SLOTS + TAIL
-    row = (slot // SIDE) * stride + (slot % SIDE) * CAP + position
-    at = position[:, None] == jnp.arange(CAP, dtype=jnp.int32)[None, :]
-    placed = lax.dot_general(
-        matches,
-        jnp.where(at, (label + 1).astype(jnp.float32)[:, None], 0.0),
-        (((0,), (0,)), ((), ())),
-        preferred_element_type=jnp.float32,
-    )
-    share = LANES // CAP
-    group = (lax.axis_index("yb") * 2 + lax.axis_index("c")) % share
-    lanes = jnp.arange(LANES, dtype=jnp.int32)[None, None, :] // CAP == group
-    tags = jnp.where(lanes, jnp.tile(placed.reshape(GROUPS, SIDE, CAP), (1, 1, share)), 0.0)
-    tags = jnp.pad(tags, ((0, 0), (0, TAIL - SIDE), (0, 0)))
-
-    packed = pack(row, points, tags)
+    width = points.shape[1]
+    group = (lax.axis_index("yb") * 2 + lax.axis_index("c")) % (LANES // CAP)
+    packed = pack(group.reshape(1), assignment, points)
     met = lax.all_to_all(packed, ("zb", "x", "yb", "c"), split_axis=0, concat_axis=0, tiled=True)
     partial = merge(met)
-    partial = lax.all_to_all(partial, ("yp", "zp"), split_axis=0, concat_axis=0, tiled=True)
+    partial = lax.all_to_all(partial, ("zp", "yp"), split_axis=0, concat_axis=0, tiled=True)
     offset = (lax.axis_index("zp") * ROWS % LANES).reshape(1)
     done = finish(offset, partial)
     gathered = lax.all_gather(done, ("zp", "zb"), axis=0, tiled=False)

time: 189 us -> 191 us (1.011)
  waiting for transfers between devices: 49.9 us -> 53.1 us
  Pallas kernels: 12.6 us -> 14.7 us
    all_to_all x1, waiting for transfers between devices: 49.9 us -> 53.1 us  [body(): lax.all_to_all(partial, ('zp', 'yp'), split_axis=0, concat_axis=0, tiled=...]
    pallas_call x1, Pallas kernels: 5.06 us -> 7.16 us  [pack(): pl.pallas_call(pack_kernel, out_shape=jax.ShapeDtypeStruct((MERGE * strid...]
where the time goes in v5:
time: 191 us
  blocking collectives  109 us (57%)
  waiting for transfers between devices  53.1 us (28%)
  Pallas kernels  14.7 us (8%)
  starting transfers between devices  12.8 us (7%)
    all_to_all x1, blocking collectives, body(): lax.all_to_all(packed, ('zb', 'x', 'yb', 'c'), split_axis=0, concat_axis=...  82.4 us
    all_to_all x1, waiting for transfers between devices, body(): lax.all_to_all(partial, ('zp', 'yp'), split_axis=0, concat_axis=0, tiled=...  53.1 us
    all_gather x1, blocking collectives, body(): gathered = lax.all_gather(done, ('zp', 'zb'), axis=0, tiled=False)  26.2 us
    all_to_all x1, starting transfers between devices, body(): lax.all_to_all(partial, ('zp', 'yp'), split_axis=0, concat_axis=0, tiled=...  12.8 us
    pallas_call x1, Pallas kernels, pack(): pl.pallas_call(pack_kernel, out_shape=jax.ShapeDtypeStruct((MERGE * strid...  7.16 us
    pallas_call x1, Pallas kernels, merge(): pl.pallas_call(merge_kernel, out_shape=jax.ShapeDtypeStruct((SIDE * SIDE,...  6.4 us
  transfers between devices with their start and end apart: 1, of which 1 were waited for; matrix products, arithmetic and copies ran while one was open for 0% of the time, Pallas kernels for 0%

profile of v5, /device:TPU:2, one launch (start us, length us, event | category | flops | bytes accessed | tf_op | source)
XLA Modules:
  0.0 190.5 jit_solution(10915919365968862433)
XLA Ops:
  0.6 0.0 copy-start
  0.7 0.7 copy-done
  1.3 7.2 %pack.1 = f32[12544,128]{1,0:T(8,128)S(1)} custom-call(s32[1]{0:T(128)} %bitcast.1.group_ref, s32[8,128]{1,0:T(8,128)S(1)} %bitcast.8, f32[1024,768]{1,0:T(8,128)} %given_ref.1), custom_call_target="tpu_custom_call" | custom-call | tf_op jit(solution)/shard_map/pack/pallas_call | solution.py:122
  8.5 82.4 %all_to_all.10.arrived_ref = f32[32,392,128]{2,1,0:T(8,128)S(1)} all-to-all(f32[32,392,128]{2,1,0:T(8,128)S(1)} %bitcast.6), channel_id=1, replica_groups=mesh['zp'=4,'zb'=2,'x'=4,'yp'=4,'yb'=2,'c'=2] {'zb','x','yb','c'}, dimensions={0} | all-to-all | bytes 12845056 | tf_op jit(solution)/shard_map/all_to_all | solution.py:277
  90.9 6.4 %merge.1 = f32[16,200,128]{2,1,0:T(8,128)} custom-call(f32[32,392,128]{2,1,0:T(8,128)S(1)} %all_to_all.10.arrived_ref), custom_call_target="tpu_custom_call" | custom-call | tf_op jit(solution)/shard_map/merge/pallas_call | solution.py:190
  97.3 12.8 %all-to-all-start.1 = ((f32[16,200,128]{2,1,0:T(8,128)}), f32[16,200,128]{2,1,0:T(8,128)S(1)}, u32[]{:S(2)}, u32[]{:S(2)}) async-start(f32[16,200,128]{2,1,0:T(8,128)} %merge.1), calls=%async_computation.1 | async-start | bytes 3276800 | tf_op jit(solution)/shard_map/all_to_all | solution.py:279
  110.1 53.1 %all-to-all-done.1.arrived_ref = f32[16,200,128]{2,1,0:T(8,128)S(1)} async-done(((f32[16,200,128]{2,1,0:T(8,128)}), f32[16,200,128]{2,1,0:T(8,128)S(1)}, u32[]{:S(2)}, u32[]{:S(2)}) %all-to-all-start.1) | async-done | bytes 1638432 | tf_op jit(solution)/shard_map/all_to_all | solution.py:279
  163.2 0.2 finish.1
  163.4 26.2 %all-gather = f32[1600,128]{1,0:T(8,128)S(1)} all-gather(f32[200,128]{1,0:T(8,128)S(1)} %finish.1), channel_id=2, replica_groups=mesh['zp'=4,'zb'=2,'x'=4,'yp'=4,'yb'=2,'c'=2] {'zp','zb'}, dimensions={0}, use_global_device_ids=true | all-gather | bytes 921600 | tf_op jit(solution)/shard_map/all_gather | solution.py:282
  189.6 0.9 lay.1
Async XLA Ops:
  0.6 0.7 copy-start
  97.3 65.9 %all-to-all-start.1 = ((f32[16,200,128]{2,1,0:T(8,128)}), f32[16,200,128]{2,1,0:T(8,128)S(1)}, u32[]{:S(2)}, u32[]{:S(2)}) async-start(f32[16,200,128]{2,1,0:T(8,128)} %merge.1), calls=%async_computation.1 | async-start | bytes 3276800 | tf_op jit(solution)/shard_map/all_to_all | solution.py:279

commit v6 on v5

--- a/solution.py
+++ b/solution.py
@@ -18,7 +18,7 @@
 ROWS = CL_OWN // SIDE
 KEYS = MERGE * CAP
 TAIL = 8
-PIECES = 4
+PIECES = 2
 PACK_MIB = 12
 
 
@@ -97,22 +97,22 @@
     listing.wait()
 
     def put(i, carry):
-        start = pl.multiple_of(i * 8, 8)
-        line = i >> 4
-        first = (i & 15) * 8
-        ats = [at_ref[line, first + r] for r in range(8)]
-        for h in range(HALVES):
-            for j in range(blocks):
-                low = (h * blocks + j) * LANES
-                tile = points_ref[pl.ds(start, 8), low : low + LANES]
-                for r in range(8):
-                    at = ats[r] + (h * GROUPS * stride + j * SLOTS)
-                    flat[pl.ds(at, 1), :] = tile[r : r + 1]
+        start = pl.multiple_of(i * LANES, LANES)
+        for first in range(0, LANES, 8):
+            ats = [at_ref[i, first + r] for r in range(8)]
+            for h in range(HALVES):
+                for j in range(blocks):
+                    low = (h * blocks + j) * LANES
+                    tile = points_ref[pl.ds(start + first, 8), low : low + LANES]
+                    for r in range(8):
+                        at = ats[r] + (h * GROUPS * stride + j * SLOTS)
+                        flat[pl.ds(at, 1), :] = tile[r : r + 1]
         return carry
 
+    lines = piece // LANES
     for k, copy in enumerate(copies):
         copy.wait()
-        lax.fori_loop(k * piece // 8, (k + 1) * piece // 8, put, 0)
+        lax.fori_loop(k * lines, (k + 1) * lines, put, 0)
 
 
 def pack(group, assignment, points):
@@ -160,7 +160,7 @@
             total = jnp.dot(hot_ref[m], terms, preferred_element_type=jnp.float32)
             total = total[:, 2 * LANES :] + total[:, LANES : 2 * LANES] + total[:, :LANES]
             for zp in range(SIDE):
-                out_ref[zp * SIDE + m, j * ROWS : (j + 1) * ROWS, :] = total[
+                out_ref[m * SIDE + zp, j * ROWS : (j + 1) * ROWS, :] = total[
                     zp * ROWS : (zp + 1) * ROWS
                 ]
         ones = jnp.ones((TAIL, LANES), jnp.bfloat16)
@@ -182,7 +182,7 @@
         )
         for zp in range(SIDE):
             low = zp * ROWS // LANES * LANES
-            out_ref[zp * SIDE + m, blocks * ROWS :, :] = small[:, low : low + LANES]
+            out_ref[m * SIDE + zp, blocks * ROWS :, :] = small[:, low : low + LANES]
 
 
 def merge(arrived):
@@ -276,7 +276,7 @@
     packed = pack(group.reshape(1), assignment, points)
     met = lax.all_to_all(packed, ("zb", "x", "yb", "c"), split_axis=0, concat_axis=0, tiled=True)
     partial = merge(met)
-    partial = lax.all_to_all(partial, ("zp", "yp"), split_axis=0, concat_axis=0, tiled=True)
+    partial = lax.all_to_all(partial, ("yp", "zp"), split_axis=0, concat_axis=0, tiled=True)
     offset = (lax.axis_index("zp") * ROWS % LANES).reshape(1)
     done = finish(offset, partial)
     gathered = lax.all_gather(done, ("zp", "zb"), axis=0, tiled=False)

time: 191 us -> 186 us (0.974)
  waiting for transfers between devices: 53.1 us -> 50.3 us
  Pallas kernels: 14.7 us -> 12.7 us
    all_to_all x1, waiting for transfers between devices: 53.1 us -> 50.3 us  [body(): lax.all_to_all(partial, ('yp', 'zp'), split_axis=0, concat_axis=0, tiled=...]
    pallas_call x1, Pallas kernels: 7.16 us -> 5.18 us  [pack(): pl.pallas_call(pack_kernel, out_shape=jax.ShapeDtypeStruct((MERGE * strid...]
where the time goes in v6:
time: 186 us
  blocking collectives  108 us (58%)
  waiting for transfers between devices  50.3 us (27%)
  starting transfers between devices  12.8 us (7%)
  Pallas kernels  12.7 us (7%)
    all_to_all x1, blocking collectives, body(): lax.all_to_all(packed, ('zb', 'x', 'yb', 'c'), split_axis=0, concat_axis=...  82.4 us
    all_to_all x1, waiting for transfers between devices, body(): lax.all_to_all(partial, ('yp', 'zp'), split_axis=0, concat_axis=0, tiled=...  50.3 us
    all_gather x1, blocking collectives, body(): gathered = lax.all_gather(done, ('zp', 'zb'), axis=0, tiled=False)  26.1 us
    all_to_all x1, starting transfers between devices, body(): lax.all_to_all(partial, ('yp', 'zp'), split_axis=0, concat_axis=0, tiled=...  12.8 us
    pallas_call x1, Pallas kernels, merge(): pl.pallas_call(merge_kernel, out_shape=jax.ShapeDtypeStruct((SIDE * SIDE,...  6.4 us
    pallas_call x1, Pallas kernels, pack(): pl.pallas_call(pack_kernel, out_shape=jax.ShapeDtypeStruct((MERGE * strid...  5.18 us
  transfers between devices with their start and end apart: 1, of which 1 were waited for; matrix products, arithmetic and copies ran while one was open for 0% of the time, Pallas kernels for 0%

profile of v6, /device:TPU:2, one launch (start us, length us, event | category | flops | bytes accessed | tf_op | source)
XLA Modules:
  0.0 185.6 jit_solution(4519150005050091124)
XLA Ops:
  0.6 0.0 copy-start
  0.7 0.7 copy-done
  1.3 5.2 %pack.1 = f32[12544,128]{1,0:T(8,128)S(1)} custom-call(s32[1]{0:T(128)} %bitcast.1.group_ref, s32[8,128]{1,0:T(8,128)S(1)} %bitcast.8, f32[1024,768]{1,0:T(8,128)} %given_ref.1), custom_call_target="tpu_custom_call" | custom-call | tf_op jit(solution)/shard_map/pack/pallas_call | solution.py:122
  6.5 82.4 %all_to_all.10.arrived_ref = f32[32,392,128]{2,1,0:T(8,128)S(1)} all-to-all(f32[32,392,128]{2,1,0:T(8,128)S(1)} %bitcast.6), channel_id=1, replica_groups=mesh['zp'=4,'zb'=2,'x'=4,'yp'=4,'yb'=2,'c'=2] {'zb','x','yb','c'}, dimensions={0} | all-to-all | bytes 12845056 | tf_op jit(solution)/shard_map/all_to_all | solution.py:277
  88.9 6.4 %merge.1 = f32[16,200,128]{2,1,0:T(8,128)} custom-call(f32[32,392,128]{2,1,0:T(8,128)S(1)} %all_to_all.10.arrived_ref), custom_call_target="tpu_custom_call" | custom-call | tf_op jit(solution)/shard_map/merge/pallas_call | solution.py:190
  95.3 12.8 %all-to-all-start.1 = ((f32[16,200,128]{2,1,0:T(8,128)}), f32[16,200,128]{2,1,0:T(8,128)S(1)}, u32[]{:S(2)}, u32[]{:S(2)}) async-start(f32[16,200,128]{2,1,0:T(8,128)} %merge.1), calls=%async_computation.1 | async-start | bytes 3276800 | tf_op jit(solution)/shard_map/all_to_all | solution.py:279
  108.1 50.3 %all-to-all-done.1.arrived_ref = f32[16,200,128]{2,1,0:T(8,128)S(1)} async-done(((f32[16,200,128]{2,1,0:T(8,128)}), f32[16,200,128]{2,1,0:T(8,128)S(1)}, u32[]{:S(2)}, u32[]{:S(2)}) %all-to-all-start.1) | async-done | bytes 1638432 | tf_op jit(solution)/shard_map/all_to_all | solution.py:279
  158.5 0.2 finish.1
  158.6 26.1 %all-gather = f32[1600,128]{1,0:T(8,128)S(1)} all-gather(f32[200,128]{1,0:T(8,128)S(1)} %finish.1), channel_id=2, replica_groups=mesh['zp'=4,'zb'=2,'x'=4,'yp'=4,'yb'=2,'c'=2] {'zp','zb'}, dimensions={0}, use_global_device_ids=true | all-gather | bytes 921600 | tf_op jit(solution)/shard_map/all_gather | solution.py:282
  184.7 0.9 lay.1
Async XLA Ops:
  0.6 0.7 copy-start
  95.3 63.2 %all-to-all-start.1 = ((f32[16,200,128]{2,1,0:T(8,128)}), f32[16,200,128]{2,1,0:T(8,128)S(1)}, u32[]{:S(2)}, u32[]{:S(2)}) async-start(f32[16,200,128]{2,1,0:T(8,128)} %merge.1), calls=%async_computation.1 | async-start | bytes 3276800 | tf_op jit(solution)/shard_map/all_to_all | solution.py:279

commit v7 on v6

--- a/solution.py
+++ b/solution.py
@@ -38,7 +38,7 @@
     return pltpu.CompilerParams(vmem_limit_bytes=mib * 1024 * 1024)
 
 
-def pack_kernel(group_ref, assignment_ref, given_ref, flat, points_ref, rows_ref, at_ref, sems):
+def pack_kernel(here_ref, assignment_ref, given_ref, flat, points_ref, rows_ref, at_ref, sems):
     rows, width = points_ref.shape
     piece = rows // PIECES
     copies = [
@@ -72,7 +72,7 @@
         position = jnp.sum(hot * (before + seen), axis=0, keepdims=True).astype(jnp.int32)
         seen = seen + jnp.sum(hot, axis=1, keepdims=True)
         rows_ref[i : i + 1, :] = group * stride + member * CAP + position
-        at = (place == position + group_ref[0] * CAP).astype(jnp.float32)
+        at = (place == position + (here_ref[0] >> 7) * CAP).astype(jnp.float32)
         tags = tags + lax.dot_general(
             (hot * label.astype(jnp.float32)).astype(jnp.bfloat16),
             at.astype(jnp.bfloat16),
@@ -115,7 +115,7 @@
         lax.fori_loop(k * lines, (k + 1) * lines, put, 0)
 
 
-def pack(group, assignment, points):
+def pack(here, assignment, points):
     rows, width = points.shape
     stride = width // LANES // HALVES * SLOTS + TAIL
     lines = (rows // LANES, LANES)
@@ -132,7 +132,7 @@
         ],
         compiler_params=params(PACK_MIB),
         name="pack",
-    )(group, assignment.reshape(lines), pltpu.with_memory_space_constraint(points, pltpu.HBM))
+    )(here, assignment.reshape(lines), pltpu.with_memory_space_constraint(points, pltpu.HBM))
     return packed.reshape(MERGE, stride, LANES)
 
 
@@ -201,39 +201,43 @@
     )(arrived)
 
 
-def finish_kernel(offset_ref, arrived_ref, out_ref):
+def finish_kernel(here_ref, arrived_ref, out_ref):
     total = arrived_ref[0]
     for k in range(1, SIDE * SIDE):
         total = total + arrived_ref[k]
     tail = total.shape[0] - TAIL
     row = lax.broadcasted_iota(jnp.int32, (ROWS, LANES), 0)
     lane = lax.broadcasted_iota(jnp.int32, (ROWS, LANES), 1)
-    mine = lane == row + offset_ref[0]
+    mine = lane == row + (here_ref[0] & (LANES - 1))
     counts = jnp.sum(jnp.where(mine, total[tail : tail + 1], 0.0), axis=1, keepdims=True)
     denom = jnp.maximum(counts, 1.0)
     norm = jnp.zeros((ROWS, LANES), jnp.float32)
     for low in range(0, tail, ROWS):
         sums = total[low : low + ROWS]
         norm = norm + sums * sums
-        out_ref[low : low + ROWS, :] = sums / denom
+        means = sums / denom
+        for k in range(SIDE * HALVES):
+            out_ref[k, low : low + ROWS, :] = means
     norm = jnp.sum(norm, axis=1, keepdims=True)
     norm = jnp.sum(jnp.where(mine, norm, 0.0), axis=0, keepdims=True)
     squares = total[tail + 1 : tail + 2] + total[tail + 2 : tail + 3] + total[tail + 3 : tail + 4]
     line = lax.broadcasted_iota(jnp.int32, (TAIL, LANES), 0)
     last = jnp.where(line == 0, total[tail : tail + 1], 0.0)
     last = jnp.where(line == 1, squares, last)
-    out_ref[tail:, :] = jnp.where(line == 2, norm, last)
-
-
-def finish(offset, arrived):
+    last = jnp.where(line == 2, norm, last)
+    for k in range(SIDE * HALVES):
+        out_ref[k, tail:, :] = last
+
+
+def finish(here, arrived):
     return pl.pallas_call(
         finish_kernel,
-        out_shape=jax.ShapeDtypeStruct(arrived.shape[1:], jnp.float32),
+        out_shape=jax.ShapeDtypeStruct((SIDE * HALVES, *arrived.shape[1:]), jnp.float32),
         in_specs=[whole(pltpu.SMEM), whole()],
         out_specs=whole(),
         compiler_params=params(6),
         name="finish",
-    )(offset, arrived)
+    )(here, arrived)
 
 
 def lay_kernel(all_ref, centre_ref, spread_ref):
@@ -273,13 +277,14 @@
 def body(points, assignment):
     width = points.shape[1]
     group = (lax.axis_index("yb") * 2 + lax.axis_index("c")) % (LANES // CAP)
-    packed = pack(group.reshape(1), assignment, points)
+    offset = lax.axis_index("zp") * ROWS % LANES
+    here = (group * LANES + offset).reshape(1)
+    packed = pack(here, assignment, points)
     met = lax.all_to_all(packed, ("zb", "x", "yb", "c"), split_axis=0, concat_axis=0, tiled=True)
     partial = merge(met)
     partial = lax.all_to_all(partial, ("yp", "zp"), split_axis=0, concat_axis=0, tiled=True)
-    offset = (lax.axis_index("zp") * ROWS % LANES).reshape(1)
-    done = finish(offset, partial)
-    gathered = lax.all_gather(done, ("zp", "zb"), axis=0, tiled=False)
+    done = finish(here, partial)
+    gathered = lax.all_to_all(done, ("zp", "zb"), split_axis=0, concat_axis=0, tiled=True)
     centre, spread = lay(gathered, width)
     return centre, spread.reshape(CL_OWN)
 

time: 186 us -> 183 us (0.984)
  the two profiles are of different devices: /device:TPU:2 before, /device:TPU:4 now
where the time goes in v7:
time: 183 us
  blocking collectives  170 us (93%)
  Pallas kernels  11.5 us (6%)
    all_to_all x1, blocking collectives, body(): lax.all_to_all(packed, ('zb', 'x', 'yb', 'c'), split_axis=0, concat_axis=...  81.9 us
    all_to_all x1, blocking collectives, body(): lax.all_to_all(partial, ('yp', 'zp'), split_axis=0, concat_axis=0, tiled=...  62.5 us
    all_to_all x1, blocking collectives, body(): lax.all_to_all(done, ('zp', 'zb'), split_axis=0, concat_axis=0, tiled=True)  25.3 us
    pallas_call x1, Pallas kernels, merge(): pl.pallas_call(merge_kernel, out_shape=jax.ShapeDtypeStruct((SIDE * SIDE,...  5.19 us
    pallas_call x1, Pallas kernels, pack(): pl.pallas_call(pack_kernel, out_shape=jax.ShapeDtypeStruct((MERGE * strid...  5.18 us

profile of v7, /device:TPU:4, one launch (start us, length us, event | category | flops | bytes accessed | tf_op | source)
XLA Modules:
  0.0 182.6 jit_solution(2573088154558396875)
XLA Ops:
  0.7 0.0 copy-start
  0.7 0.7 copy-done
  1.3 5.2 %pack.1 = f32[12544,128]{1,0:T(8,128)S(1)} custom-call(s32[1]{0:T(128)} %bitcast.here_ref, s32[8,128]{1,0:T(8,128)S(1)} %bitcast.5, f32[1024,768]{1,0:T(8,128)} %given_ref.1), custom_call_target="tpu_custom_call" | custom-call | tf_op jit(solution)/shard_map/pack/pallas_call | solution.py:122
  6.5 81.9 %all_to_all.15.arrived_ref = f32[32,392,128]{2,1,0:T(8,128)S(1)} all-to-all(f32[32,392,128]{2,1,0:T(8,128)S(1)} %bitcast.4), channel_id=1, replica_groups=mesh['zp'=4,'zb'=2,'x'=4,'yp'=4,'yb'=2,'c'=2] {'zb','x','yb','c'}, dimensions={0} | all-to-all | bytes 12845056 | tf_op jit(solution)/shard_map/all_to_all | solution.py:283
  88.4 5.2 %merge.1 = f32[16,200,128]{2,1,0:T(8,128)S(1)} custom-call(f32[32,392,128]{2,1,0:T(8,128)S(1)} %all_to_all.15.arrived_ref), custom_call_target="tpu_custom_call" | custom-call | tf_op jit(solution)/shard_map/merge/pallas_call | solution.py:190
  93.6 62.5 %all_to_all.16.arrived_ref = f32[16,200,128]{2,1,0:T(8,128)S(1)} all-to-all(f32[16,200,128]{2,1,0:T(8,128)S(1)} %merge.1), channel_id=1, replica_groups=mesh['zp'=4,'zb'=2,'x'=4,'yp'=4,'yb'=2,'c'=2] {'yp','zp'}, dimensions={0} | all-to-all | bytes 3276800 | tf_op jit(solution)/shard_map/all_to_all | solution.py:285
  156.1 0.2 finish.1
  156.3 25.3 %all_to_all.17.all_ref = f32[8,200,128]{2,1,0:T(8,128)S(1)} all-to-all(f32[8,200,128]{2,1,0:T(8,128)S(1)} %finish.1), channel_id=1, replica_groups=mesh['zp'=4,'zb'=2,'x'=4,'yp'=4,'yb'=2,'c'=2] {'zp','zb'}, dimensions={0} | all-to-all | bytes 1638400 | tf_op jit(solution)/shard_map/all_to_all | solution.py:287
  181.6 0.9 lay.1
Async XLA Ops:
  0.7 0.7 copy-start

commit v8 on v7

--- a/solution.py
+++ b/solution.py
@@ -100,13 +100,14 @@
         start = pl.multiple_of(i * LANES, LANES)
         for first in range(0, LANES, 8):
             ats = [at_ref[i, first + r] for r in range(8)]
-            for h in range(HALVES):
-                for j in range(blocks):
-                    low = (h * blocks + j) * LANES
-                    tile = points_ref[pl.ds(start + first, 8), low : low + LANES]
-                    for r in range(8):
-                        at = ats[r] + (h * GROUPS * stride + j * SLOTS)
-                        flat[pl.ds(at, 1), :] = tile[r : r + 1]
+            tiles = [
+                points_ref[pl.ds(start + first, 8), k * LANES : (k + 1) * LANES]
+                for k in range(HALVES * blocks)
+            ]
+            for r in range(8):
+                for k, tile in enumerate(tiles):
+                    at = ats[r] + (k // blocks * GROUPS * stride + k % blocks * SLOTS)
+                    flat[pl.ds(at, 1), :] = tile[r : r + 1]
         return carry
 
     lines = piece // LANES
@@ -146,19 +147,22 @@
         for s in range(1, gather):
             tile = tile + arrived_ref[k * gather + s, tail:, :]
         tiles.append(tile)
-    tags = jnp.concatenate(tiles, axis=1).astype(jnp.int32)
+    tags = jnp.concatenate(tiles, axis=1).astype(jnp.bfloat16)
     cluster = lax.broadcasted_iota(jnp.int32, (CL_OWN, KEYS), 0) + 1
+    cluster = cluster.astype(jnp.float32).astype(jnp.bfloat16)
+    one = jnp.ones((CL_OWN, KEYS), jnp.bfloat16)
+    none = jnp.zeros((CL_OWN, KEYS), jnp.bfloat16)
     for m in range(SIDE):
-        hot = (cluster == tags[m : m + 1]).astype(jnp.float32).astype(jnp.bfloat16)
+        hot = jnp.where(cluster == tags[m : m + 1], one, none)
         hot_ref[m] = hot
         for j in range(blocks):
             low = j * SLOTS + m * CAP
             data = arrived_ref[:, low : low + CAP, :].reshape(KEYS, LANES)
             squares = data * data
             square_ref[...] = squares if j == 0 else square_ref[...] + squares
-            terms = jnp.concatenate(split3(data), axis=1)
+            terms = jnp.concatenate(split3(data)[:2], axis=1)
             total = jnp.dot(hot_ref[m], terms, preferred_element_type=jnp.float32)
-            total = total[:, 2 * LANES :] + total[:, LANES : 2 * LANES] + total[:, :LANES]
+            total = total[:, LANES:] + total[:, :LANES]
             for zp in range(SIDE):
                 out_ref[m * SIDE + zp, j * ROWS : (j + 1) * ROWS, :] = total[
                     zp * ROWS : (zp + 1) * ROWS

time: 183 us -> 180 us (0.984)
  Pallas kernels: 11.5 us -> 8.49 us
where the time goes in v8:
time: 180 us
  blocking collectives  170 us (94%)
  Pallas kernels  8.49 us (5%)
    all_to_all x1, blocking collectives, body(): lax.all_to_all(packed, ('zb', 'x', 'yb', 'c'), split_axis=0, concat_axis=...  81.9 us
    all_to_all x1, blocking collectives, body(): lax.all_to_all(partial, ('yp', 'zp'), split_axis=0, concat_axis=0, tiled=...  62.7 us
    all_to_all x1, blocking collectives, body(): lax.all_to_all(done, ('zp', 'zb'), split_axis=0, concat_axis=0, tiled=True)  25.3 us
    pallas_call x1, Pallas kernels, merge(): pl.pallas_call(merge_kernel, out_shape=jax.ShapeDtypeStruct((SIDE * SIDE,...  3.76 us
    pallas_call x1, Pallas kernels, pack(): pl.pallas_call(pack_kernel, out_shape=jax.ShapeDtypeStruct((MERGE * strid...  3.63 us

profile of v8, /device:TPU:4, one launch (start us, length us, event | category | flops | bytes accessed | tf_op | source)
XLA Modules:
  0.0 179.7 jit_solution(8642802522313617076)
XLA Ops:
  0.7 0.0 copy-start
  0.7 0.7 copy-done
  1.3 3.6 %pack.1 = f32[12544,128]{1,0:T(8,128)S(1)} custom-call(s32[1]{0:T(128)} %bitcast.here_ref, s32[8,128]{1,0:T(8,128)S(1)} %bitcast.5, f32[1024,768]{1,0:T(8,128)} %given_ref.1), custom_call_target="tpu_custom_call" | custom-call | tf_op jit(solution)/shard_map/pack/pallas_call | solution.py:123
  5.0 81.9 %all_to_all.15.arrived_ref = f32[32,392,128]{2,1,0:T(8,128)S(1)} all-to-all(f32[32,392,128]{2,1,0:T(8,128)S(1)} %bitcast.4), channel_id=1, replica_groups=mesh['zp'=4,'zb'=2,'x'=4,'yp'=4,'yb'=2,'c'=2] {'zb','x','yb','c'}, dimensions={0} | all-to-all | bytes 12845056 | tf_op jit(solution)/shard_map/all_to_all | solution.py:287
  86.9 3.8 %merge.1 = f32[16,200,128]{2,1,0:T(8,128)S(1)} custom-call(f32[32,392,128]{2,1,0:T(8,128)S(1)} %all_to_all.15.arrived_ref), custom_call_target="tpu_custom_call" | custom-call | tf_op jit(solution)/shard_map/merge/pallas_call | solution.py:194
  90.6 62.7 %all_to_all.16.arrived_ref = f32[16,200,128]{2,1,0:T(8,128)S(1)} all-to-all(f32[16,200,128]{2,1,0:T(8,128)S(1)} %merge.1), channel_id=1, replica_groups=mesh['zp'=4,'zb'=2,'x'=4,'yp'=4,'yb'=2,'c'=2] {'yp','zp'}, dimensions={0} | all-to-all | bytes 3276800 | tf_op jit(solution)/shard_map/all_to_all | solution.py:289
  153.3 0.2 finish.1
  153.5 25.3 %all_to_all.17.all_ref = f32[8,200,128]{2,1,0:T(8,128)S(1)} all-to-all(f32[8,200,128]{2,1,0:T(8,128)S(1)} %finish.1), channel_id=1, replica_groups=mesh['zp'=4,'zb'=2,'x'=4,'yp'=4,'yb'=2,'c'=2] {'zp','zb'}, dimensions={0} | all-to-all | bytes 1638400 | tf_op jit(solution)/shard_map/all_to_all | solution.py:291
  178.8 0.9 lay.1
Async XLA Ops:
  0.7 0.7 copy-start

commit v9 on v8

--- a/solution.py
+++ b/solution.py
@@ -71,7 +71,7 @@
         )
         position = jnp.sum(hot * (before + seen), axis=0, keepdims=True).astype(jnp.int32)
         seen = seen + jnp.sum(hot, axis=1, keepdims=True)
-        rows_ref[i : i + 1, :] = group * stride + member * CAP + position
+        rows_ref[i : i + 1, :] = group * (HALVES * stride) + member * CAP + position
         at = (place == position + (here_ref[0] >> 7) * CAP).astype(jnp.float32)
         tags = tags + lax.dot_general(
             (hot * label.astype(jnp.float32)).astype(jnp.bfloat16),
@@ -84,7 +84,7 @@
 
     for g in range(MERGE):
         low = (g + 1) * stride - TAIL
-        owners = (g % GROUPS) * SIDE
+        owners = g // HALVES * SIDE
         flat[low : low + SIDE, :] = tags[owners : owners + SIDE]
         flat[low + SIDE : low + TAIL, :] = jnp.zeros((TAIL - SIDE, LANES), jnp.float32)
 
@@ -106,7 +106,7 @@
             ]
             for r in range(8):
                 for k, tile in enumerate(tiles):
-                    at = ats[r] + (k // blocks * GROUPS * stride + k % blocks * SLOTS)
+                    at = ats[r] + (k // blocks * stride + k % blocks * SLOTS)
                     flat[pl.ds(at, 1), :] = tile[r : r + 1]
         return carry
 
@@ -280,11 +280,11 @@
 
 def body(points, assignment):
     width = points.shape[1]
-    group = (lax.axis_index("yb") * 2 + lax.axis_index("c")) % (LANES // CAP)
+    group = (lax.axis_index("c") * HALVES + lax.axis_index("zb")) % (LANES // CAP)
     offset = lax.axis_index("zp") * ROWS % LANES
     here = (group * LANES + offset).reshape(1)
     packed = pack(here, assignment, points)
-    met = lax.all_to_all(packed, ("zb", "x", "yb", "c"), split_axis=0, concat_axis=0, tiled=True)
+    met = lax.all_to_all(packed, ("x", "yb", "c", "zb"), split_axis=0, concat_axis=0, tiled=True)
     partial = merge(met)
     partial = lax.all_to_all(partial, ("yp", "zp"), split_axis=0, concat_axis=0, tiled=True)
     done = finish(here, partial)

time: 180 us -> 185 us (1.028)
  the two profiles are of different devices: /device:TPU:4 before, /device:TPU:2 now
where the time goes in v9:
time: 185 us; the launch traced here: 184 us
  blocking collectives  175 us (95%)
  Pallas kernels  8.43 us (5%)
    all_to_all x1, blocking collectives, body(): lax.all_to_all(packed, ('x', 'yb', 'c', 'zb'), split_axis=0, concat_axis=...  82.1 us
    all_to_all x1, blocking collectives, body(): lax.all_to_all(partial, ('yp', 'zp'), split_axis=0, concat_axis=0, tiled=...  66.4 us
    all_to_all x1, blocking collectives, body(): lax.all_to_all(done, ('zp', 'zb'), split_axis=0, concat_axis=0, tiled=True)  26.1 us
    pallas_call x1, Pallas kernels, merge(): pl.pallas_call(merge_kernel, out_shape=jax.ShapeDtypeStruct((SIDE * SIDE,...  3.77 us

profile of v9, /device:TPU:2, one launch (start us, length us, event | category | flops | bytes accessed | tf_op | source)
XLA Modules:
  0.0 184.4 jit_solution(13744445392609375889)
XLA Ops:
  0.7 0.0 copy-start
  0.7 0.7 copy-done
  1.3 3.6 %pack.1 = f32[12544,128]{1,0:T(8,128)S(1)} custom-call(s32[1]{0:T(128)} %bitcast.here_ref, s32[8,128]{1,0:T(8,128)S(1)} %bitcast.5, f32[1024,768]{1,0:T(8,128)} %given_ref.1), custom_call_target="tpu_custom_call" | custom-call | tf_op jit(solution)/shard_map/pack/pallas_call | solution.py:123
  4.9 82.1 %all_to_all.15.arrived_ref = f32[32,392,128]{2,1,0:T(8,128)S(1)} all-to-all(f32[32,392,128]{2,1,0:T(8,128)S(1)} %bitcast.4), channel_id=1, replica_groups=mesh['zp'=4,'zb'=2,'x'=4,'yp'=4,'yb'=2,'c'=2] {'x','yb','c','zb'}, dimensions={0} | all-to-all | bytes 12845056 | tf_op jit(solution)/shard_map/all_to_all | solution.py:287
  87.0 3.8 %merge.1 = f32[16,200,128]{2,1,0:T(8,128)S(1)} custom-call(f32[32,392,128]{2,1,0:T(8,128)S(1)} %all_to_all.15.arrived_ref), custom_call_target="tpu_custom_call" | custom-call | tf_op jit(solution)/shard_map/merge/pallas_call | solution.py:194
  90.8 66.4 %all_to_all.16.arrived_ref = f32[16,200,128]{2,1,0:T(8,128)S(1)} all-to-all(f32[16,200,128]{2,1,0:T(8,128)S(1)} %merge.1), channel_id=1, replica_groups=mesh['zp'=4,'zb'=2,'x'=4,'yp'=4,'yb'=2,'c'=2] {'yp','zp'}, dimensions={0} | all-to-all | bytes 3276800 | tf_op jit(solution)/shard_map/all_to_all | solution.py:289
  157.1 0.2 finish.1
  157.3 26.1 %all_to_all.17.all_ref = f32[8,200,128]{2,1,0:T(8,128)S(1)} all-to-all(f32[8,200,128]{2,1,0:T(8,128)S(1)} %finish.1), channel_id=1, replica_groups=mesh['zp'=4,'zb'=2,'x'=4,'yp'=4,'yb'=2,'c'=2] {'zp','zb'}, dimensions={0} | all-to-all | bytes 1638400 | tf_op jit(solution)/shard_map/all_to_all | solution.py:291
  183.5 0.9 lay.1
Async XLA Ops:
  0.7 0.7 copy-start

commit v10 on v8

--- a/solution.py
+++ b/solution.py
@@ -38,9 +38,13 @@
     return pltpu.CompilerParams(vmem_limit_bytes=mib * 1024 * 1024)
 
 
-def pack_kernel(here_ref, assignment_ref, given_ref, flat, points_ref, rows_ref, at_ref, sems):
+def pack_kernel(
+    here_ref, labels_ref, given_ref, flat, points_ref, assignment_ref, rows_ref, at_ref, sems
+):
     rows, width = points_ref.shape
     piece = rows // PIECES
+    fetch = pltpu.make_async_copy(labels_ref, assignment_ref, sems.at[PIECES + 1])
+    fetch.start()
     copies = [
         pltpu.make_async_copy(
             given_ref.at[pl.ds(k * piece, piece)], points_ref.at[pl.ds(k * piece, piece)], sems.at[k]
@@ -52,6 +56,14 @@
 
     blocks = width // LANES // HALVES
     stride = blocks * SLOTS + TAIL
+
+    def clear(g, carry):
+        start = pl.multiple_of(g * stride, 8)
+        flat[pl.ds(start, stride - TAIL), :] = jnp.zeros((stride - TAIL, LANES), jnp.float32)
+        return carry
+
+    lax.fori_loop(0, MERGE // 2, clear, 0)
+    fetch.wait()
     earlier = lax.broadcasted_iota(jnp.int32, (LANES, LANES), 0)
     lane = lax.broadcasted_iota(jnp.int32, (LANES, LANES), 1)
     earlier = (earlier < lane).astype(jnp.float32).astype(jnp.bfloat16)
@@ -88,12 +100,7 @@
         flat[low : low + SIDE, :] = tags[owners : owners + SIDE]
         flat[low + SIDE : low + TAIL, :] = jnp.zeros((TAIL - SIDE, LANES), jnp.float32)
 
-    def clear(g, carry):
-        start = pl.multiple_of(g * stride, 8)
-        flat[pl.ds(start, stride - TAIL), :] = jnp.zeros((stride - TAIL, LANES), jnp.float32)
-        return carry
-
-    lax.fori_loop(0, MERGE, clear, 0)
+    lax.fori_loop(MERGE // 2, MERGE, clear, 0)
     listing.wait()
 
     def put(i, carry):
@@ -123,17 +130,18 @@
     packed = pl.pallas_call(
         pack_kernel,
         out_shape=jax.ShapeDtypeStruct((MERGE * stride, LANES), jnp.float32),
-        in_specs=[whole(pltpu.SMEM), whole(), whole(pltpu.HBM)],
+        in_specs=[whole(pltpu.SMEM), whole(pltpu.HBM), whole(pltpu.HBM)],
         out_specs=whole(),
         scratch_shapes=[
             pltpu.VMEM(points.shape, jnp.float32),
             pltpu.VMEM(lines, jnp.int32),
+            pltpu.VMEM(lines, jnp.int32),
             pltpu.SMEM(lines, jnp.int32),
-            pltpu.SemaphoreType.DMA((PIECES + 1,)),
+            pltpu.SemaphoreType.DMA((PIECES + 2,)),
         ],
         compiler_params=params(PACK_MIB),
         name="pack",
-    )(here, assignment.reshape(lines), pltpu.with_memory_space_constraint(points, pltpu.HBM))
+    )(here, pltpu.with_memory_space_constraint(assignment.reshape(lines), pltpu.HBM), pltpu.with_memory_space_constraint(points, pltpu.HBM))
     return packed.reshape(MERGE, stride, LANES)
 
 

time: 180 us -> 179 us (level)
  no operation moved by 1% of the time
where the time goes in v10:
time: 179 us
  blocking collectives  170 us (95%)
  Pallas kernels  8.4 us (5%)
    all_to_all x1, blocking collectives, body(): lax.all_to_all(packed, ('zb', 'x', 'yb', 'c'), split_axis=0, concat_axis=...  81.9 us
    all_to_all x1, blocking collectives, body(): lax.all_to_all(partial, ('yp', 'zp'), split_axis=0, concat_axis=0, tiled=...  62.5 us
    all_to_all x1, blocking collectives, body(): lax.all_to_all(done, ('zp', 'zb'), split_axis=0, concat_axis=0, tiled=True)  25.4 us
    pallas_call x1, Pallas kernels, merge(): pl.pallas_call(merge_kernel, out_shape=jax.ShapeDtypeStruct((SIDE * SIDE,...  3.76 us

profile of v10, /device:TPU:4, one launch (start us, length us, event | category | flops | bytes accessed | tf_op | source)
XLA Modules:
  0.0 178.8 jit_solution(16949451442295508487)
XLA Ops:
  0.7 3.5 %pack.1 = f32[12544,128]{1,0:T(8,128)S(1)} custom-call(s32[1]{0:T(128)} %bitcast.here_ref, s32[8,128]{1,0:T(8,128)} %bitcast.5, f32[1024,768]{1,0:T(8,128)} %given_ref.1), custom_call_target="tpu_custom_call" | custom-call | tf_op jit(solution)/shard_map/pack/pallas_call | solution.py:130
  4.2 81.9 %all_to_all.15.arrived_ref = f32[32,392,128]{2,1,0:T(8,128)S(1)} all-to-all(f32[32,392,128]{2,1,0:T(8,128)S(1)} %bitcast.4), channel_id=1, replica_groups=mesh['zp'=4,'zb'=2,'x'=4,'yp'=4,'yb'=2,'c'=2] {'zb','x','yb','c'}, dimensions={0} | all-to-all | bytes 12845056 | tf_op jit(solution)/shard_map/all_to_all | solution.py:295
  86.1 3.8 %merge.1 = f32[16,200,128]{2,1,0:T(8,128)S(1)} custom-call(f32[32,392,128]{2,1,0:T(8,128)S(1)} %all_to_all.15.arrived_ref), custom_call_target="tpu_custom_call" | custom-call | tf_op jit(solution)/shard_map/merge/pallas_call | solution.py:202
  89.8 62.5 %all_to_all.16.arrived_ref = f32[16,200,128]{2,1,0:T(8,128)S(1)} all-to-all(f32[16,200,128]{2,1,0:T(8,128)S(1)} %merge.1), channel_id=1, replica_groups=mesh['zp'=4,'zb'=2,'x'=4,'yp'=4,'yb'=2,'c'=2] {'yp','zp'}, dimensions={0} | all-to-all | bytes 3276800 | tf_op jit(solution)/shard_map/all_to_all | solution.py:297
  152.4 0.2 finish.1
  152.5 25.4 %all_to_all.17.all_ref = f32[8,200,128]{2,1,0:T(8,128)S(1)} all-to-all(f32[8,200,128]{2,1,0:T(8,128)S(1)} %finish.1), channel_id=1, replica_groups=mesh['zp'=4,'zb'=2,'x'=4,'yp'=4,'yb'=2,'c'=2] {'zp','zb'}, dimensions={0} | all-to-all | bytes 1638400 | tf_op jit(solution)/shard_map/all_to_all | solution.py:299
  177.9 0.9 lay.1

commit v11 on v10

--- a/solution.py
+++ b/solution.py
@@ -227,24 +227,20 @@
     for low in range(0, tail, ROWS):
         sums = total[low : low + ROWS]
         norm = norm + sums * sums
-        means = sums / denom
-        for k in range(SIDE * HALVES):
-            out_ref[k, low : low + ROWS, :] = means
+        out_ref[low : low + ROWS, :] = sums / denom
     norm = jnp.sum(norm, axis=1, keepdims=True)
     norm = jnp.sum(jnp.where(mine, norm, 0.0), axis=0, keepdims=True)
     squares = total[tail + 1 : tail + 2] + total[tail + 2 : tail + 3] + total[tail + 3 : tail + 4]
     line = lax.broadcasted_iota(jnp.int32, (TAIL, LANES), 0)
     last = jnp.where(line == 0, total[tail : tail + 1], 0.0)
     last = jnp.where(line == 1, squares, last)
-    last = jnp.where(line == 2, norm, last)
-    for k in range(SIDE * HALVES):
-        out_ref[k, tail:, :] = last
+    out_ref[tail:, :] = jnp.where(line == 2, norm, last)
 
 
 def finish(here, arrived):
     return pl.pallas_call(
         finish_kernel,
-        out_shape=jax.ShapeDtypeStruct((SIDE * HALVES, *arrived.shape[1:]), jnp.float32),
+        out_shape=jax.ShapeDtypeStruct(arrived.shape[1:], jnp.float32),
         in_specs=[whole(pltpu.SMEM), whole()],
         out_specs=whole(),
         compiler_params=params(6),
@@ -296,7 +292,7 @@
     partial = merge(met)
     partial = lax.all_to_all(partial, ("yp", "zp"), split_axis=0, concat_axis=0, tiled=True)
     done = finish(here, partial)
-    gathered = lax.all_to_all(done, ("zp", "zb"), split_axis=0, concat_axis=0, tiled=True)
+    gathered = lax.all_gather(done, ("zp", "zb"), axis=0, tiled=False)
     centre, spread = lay(gathered, width)
     return centre, spread.reshape(CL_OWN)
 

time: 179 us -> 180 us (level)
    all_gather x0 -> x1, blocking collectives: none -> 26.2 us  [body(): gathered = lax.all_gather(done, ('zp', 'zb'), axis=0, tiled=False)]
    all_to_all x1 -> x0, blocking collectives: 25.4 us -> none  [body(): lax.all_to_all(done, ('zp', 'zb'), split_axis=0, concat_axis=0, tiled=True)]
where the time goes in v11:
time: 180 us
  blocking collectives  171 us (95%)
  Pallas kernels  8.4 us (5%)
    all_to_all x1, blocking collectives, body(): lax.all_to_all(packed, ('zb', 'x', 'yb', 'c'), split_axis=0, concat_axis=...  81.9 us
    all_to_all x1, blocking collectives, body(): lax.all_to_all(partial, ('yp', 'zp'), split_axis=0, concat_axis=0, tiled=...  62.7 us
    all_gather x1, blocking collectives, body(): gathered = lax.all_gather(done, ('zp', 'zb'), axis=0, tiled=False)  26.2 us
    pallas_call x1, Pallas kernels, merge(): pl.pallas_call(merge_kernel, out_shape=jax.ShapeDtypeStruct((SIDE * SIDE,...  3.76 us

profile of v11, /device:TPU:4, one launch (start us, length us, event | category | flops | bytes accessed | tf_op | source)
XLA Modules:
  0.0 179.8 jit_solution(12504364760974897131)
XLA Ops:
  0.7 3.5 %pack.1 = f32[12544,128]{1,0:T(8,128)S(1)} custom-call(s32[1]{0:T(128)} %bitcast.here_ref, s32[8,128]{1,0:T(8,128)} %bitcast.7, f32[1024,768]{1,0:T(8,128)} %given_ref.1), custom_call_target="tpu_custom_call" | custom-call | tf_op jit(solution)/shard_map/pack/pallas_call | solution.py:130
  4.2 81.9 %all_to_all.10.arrived_ref = f32[32,392,128]{2,1,0:T(8,128)S(1)} all-to-all(f32[32,392,128]{2,1,0:T(8,128)S(1)} %bitcast.5), channel_id=1, replica_groups=mesh['zp'=4,'zb'=2,'x'=4,'yp'=4,'yb'=2,'c'=2] {'zb','x','yb','c'}, dimensions={0} | all-to-all | bytes 12845056 | tf_op jit(solution)/shard_map/all_to_all | solution.py:291
  86.1 3.8 %merge.1 = f32[16,200,128]{2,1,0:T(8,128)S(1)} custom-call(f32[32,392,128]{2,1,0:T(8,128)S(1)} %all_to_all.10.arrived_ref), custom_call_target="tpu_custom_call" | custom-call | tf_op jit(solution)/shard_map/merge/pallas_call | solution.py:202
  89.8 62.7 %all_to_all.11.arrived_ref = f32[16,200,128]{2,1,0:T(8,128)S(1)} all-to-all(f32[16,200,128]{2,1,0:T(8,128)S(1)} %merge.1), channel_id=1, replica_groups=mesh['zp'=4,'zb'=2,'x'=4,'yp'=4,'yb'=2,'c'=2] {'yp','zp'}, dimensions={0} | all-to-all | bytes 3276800 | tf_op jit(solution)/shard_map/all_to_all | solution.py:293
  152.5 0.2 finish.1
  152.7 26.2 %all-gather = f32[1600,128]{1,0:T(8,128)S(1)} all-gather(f32[200,128]{1,0:T(8,128)S(1)} %finish.1), channel_id=2, replica_groups=mesh['zp'=4,'zb'=2,'x'=4,'yp'=4,'yb'=2,'c'=2] {'zp','zb'}, dimensions={0}, use_global_device_ids=true | all-gather | bytes 921600 | tf_op jit(solution)/shard_map/all_gather | solution.py:295
  178.9 0.9 lay.1
